TPU v7x, 32 devices: a whole 2x2x4 slice. The times are simulated.
32 devices in a mesh: grp: 2 (over x), row: 4 (over y, core), diag: 4 (over z).
Axes of the slice: x: 2, y: 2, z: 4, core: 2. Of those that a mesh axis runs over, the one named last changes fastest.
Arguments:
- emb_rows: bfloat16 [32, 1024], P(None, ('grp', 'row')), parts along dimension 1, may hold values from -6 to 6
- emb_cols: bfloat16 [32, 1024], P(None, ('grp', 'row')), parts along dimension 1, may hold values from -6 to 6
- kernel: bfloat16 [3, 3, 32, 32], replicated, may hold values from -0.375 to 0.375
- bias: float32 [32], replicated, may hold values from -3 to 3
- cotangent: bfloat16 [32, 1024, 512], P(None, ('grp', 'row'), 'diag'), parts along dimension 1, may hold values from -6 to 6
- valid: int32 [1024], P(('grp', 'row')), parts along dimension 0, may hold values 0 or 1
- dilation: int32 [2], P('grp'), parts along dimension 0, may hold values from 1 to 4
- band: int32 [2], P('grp'), parts along dimension 0, may hold values from 384 to 512
Outputs:
- pair_out: bfloat16 [32, 1024, 512], P(None, ('grp', 'row'), 'diag'), parts along dimension 1
- row_grad: float32 [32, 1024], P(None, ('grp', 'row')), parts along dimension 1
- col_grad: float32 [32, 1024], P(None, ('grp', 'row')), parts along dimension 1
- kernel_grad: float32 [6, 3, 32, 32], P('grp'), parts along dimension 0
- bias_grad: float32 [64], P('grp'), parts along dimension 0
There are 2 independent parts, one for each index of `grp`. A program takes and returns all parts, laid end to end along the dimension named above; an argument that names none is the same for every part. Nothing has to cross between parts.
All inputs are finite; a program needn't handle non-finite values. No bound on the sum of `valid` on one device may be relied on, other than what follows from the above.
Results may differ from a plain program's by a relative error of at most 0.0032.
Values may be sent and summed in bfloat16 or wider, within the bound.
A program may use at most 128 MiB of HBM per device.

v0:
```python
import functools

import jax
import jax.numpy as jnp
from jax import lax
from jax.experimental import pallas as pl
from jax.experimental.pallas import tpu as pltpu
from jax.sharding import PartitionSpec as P

MAXDIL = 4
RG = 8
S2PI = 0.7978845608028654
CUBIC = 0.044715


def loop(count, body):
    def step(p, c):
        body(p)
        return c
    lax.fori_loop(0, count, step, 0)


def send(src, dst, ss, sr, dq, dt):
    return pltpu.make_async_remote_copy(
        src_ref=src, dst_ref=dst, send_sem=ss, recv_sem=sr,
        device_id={"row": dq, "diag": dt}, device_id_type=pl.DeviceIdType.MESH,
    )


def gather_kernel(
    R, T, pack, cot, cols, vcol, near, ext, halo,
    blocks, edge_l, edge_r, from_r, from_l, top, bottom,
    ps, pr, hs, hr,
):
    n, ch = cot.shape[0], cot.shape[1]
    m = MAXDIL
    width = 2 * m
    per = n // width
    tiles = n // per
    q, t = lax.axis_index("row"), lax.axis_index("diag")
    bf, f32 = jnp.bfloat16, jnp.float32
    mesh_id = pl.DeviceIdType.MESH
    barrier = pltpu.get_barrier_semaphore()
    left, right, above, below = t > 0, t < T - 1, q > 0, q < R - 1

    def greet(p):
        @pl.when(p != q)
        def _():
            pl.semaphore_signal(barrier, inc=1, device_id={"row": p, "diag": t}, device_id_type=mesh_id)
    loop(R, greet)
    sides = []
    for dt, okt in ((-1, left), (1, right)):
        for dq, okq in ((-1, above), (0, True), (1, below)):
            sides.append((dq, dt, okt & okq))
    total = R - 1
    for dq, dt, ok in sides:
        total = total + jnp.where(ok, 1, 0)

        @pl.when(ok)
        def _():
            pl.semaphore_signal(barrier, inc=1, device_id={"row": q + dq, "diag": t + dt}, device_id_type=mesh_id)

    lane = lax.broadcasted_iota(jnp.int32, (ch, n), 1)

    def pack_edges(g):
        a = jnp.zeros((ch, n), f32)
        b = jnp.zeros((ch, n), f32)
        for s in range(per):
            x = cot[g * per + s].astype(f32)
            here = lane // width == s
            a = jnp.where(here, pltpu.roll(x, width * s, 1) if s else x, a)
            sh = (width * (s + 1)) % n
            b = jnp.where(here, pltpu.roll(x, sh, 1) if sh else x, b)
        edge_l[g] = a.astype(bf)
        edge_r[g] = b.astype(bf)
    loop(tiles, pack_edges)
    pl.semaphore_wait(barrier, total)

    def p1(p):
        return send(pack, blocks.at[q + 1], ps.at[p], pr.at[q], p, t)

    def halos(act):
        last = tiles - 1
        plan = (
            (left, edge_l, from_r.at[pl.ds(0, tiles)], 0, 0, -1),
            (right, edge_r, from_l.at[pl.ds(0, tiles)], 1, 0, 1),
            (above, cot.at[pl.ds(0, m)], bottom, 2, -1, 0),
            (below, cot.at[pl.ds(n - m, m)], top, 3, 1, 0),
            (below & left, edge_l.at[last], from_r.at[tiles], 4, 1, -1),
            (above & left, edge_l.at[0], from_r.at[tiles + 1], 5, -1, -1),
            (below & right, edge_r.at[last], from_l.at[tiles], 6, 1, 1),
            (above & right, edge_r.at[0], from_l.at[tiles + 1], 7, -1, 1),
        )
        flags = {(0, -1): right, (0, 1): left, (-1, 0): below, (1, 0): above,
                 (1, -1): above & right, (-1, -1): below & right, (1, 1): above & left, (-1, 1): below & left}
        for ok, src, dst, k, dq, dt in plan:
            act(ok, flags[(dq, dt)], src, dst, send(src, dst, hs.at[k], hr.at[k], q + dq, t + dt))

    def start(ok, got, src, dst, c):
        @pl.when(ok)
        def _():
            c.start()

    def peers(act):
        def one(p):
            @pl.when(p != q)
            def _():
                act(p)
        loop(R, one)

    peers(lambda p: p1(p).start())
    halos(start)

    zero = jnp.zeros(pack.shape, bf)
    blocks[0] = zero
    for k in range(R + 1, R + T + 3):
        blocks[k] = zero
    blocks[q + 1] = pack[...]

    def body_copy(g):
        for s in range(RG):
            ext[m + g * RG + s] = cot[g * RG + s]
    loop(n // RG, body_copy)

    peers(lambda p: send(pack, blocks.at[p + 1], ps.at[p], pr.at[p], q, t).wait_recv())
    rows_of = slice(ch, 2 * ch + RG)
    lane2 = lax.broadcasted_iota(jnp.int32, pack.shape, 1)
    b0, b1, b2, b3 = (blocks[q + t + k].astype(f32) for k in range(4))
    s = 28
    low = (b1, jnp.where(lane2 >= n - s, b0, b2))
    high = (jnp.where(lane2 < s, b3, b1), b2)
    for side, (x, y) in enumerate((low, high)):
        cols[side, :, :n] = x[:ch]
        cols[side, :, n:] = y[:ch]
        vcol[side, :, :n] = x[2 * ch : 2 * ch + RG]
        vcol[side, :, n:] = y[2 * ch : 2 * ch + RG]
    near[0] = blocks[q + 1].astype(f32)[rows_of]
    near[1] = jnp.where(lane2 >= n - m, blocks[q].astype(f32), blocks[q + 2].astype(f32))[rows_of]

    def finish(ok, got, src, dst, c):
        @pl.when(got)
        def _():
            c.wait_recv()

        @pl.when(jnp.logical_not(got))
        def _():
            dst[...] = jnp.zeros(dst.shape, bf)
    halos(finish)
    for s in range(m):
        ext[s] = top[s]
        ext[n + m + s] = bottom[s]

    def spread(e, tile_r, tile_l, s):
        a = pltpu.roll(tile_r, (n - width * s) % n, 1) if s else tile_r
        b = pltpu.roll(tile_l, (2 * n - width - width * s) % n, 1) if (n - width - width * s) % n else tile_l
        halo[e] = jnp.where(lane < width, a, jnp.where(lane >= n - width, b, 0.0)).astype(bf)

    def unpack(g):
        tr, tl = from_r[g].astype(f32), from_l[g].astype(f32)
        for s in range(per):
            spread(m + g * per + s, tr, tl, s)
    loop(tiles, unpack)
    tr, tl = from_r[tiles].astype(f32), from_l[tiles].astype(f32)
    for s in range(m):
        spread(s, tr, tl, per - m + s)
    tr, tl = from_r[tiles + 1].astype(f32), from_l[tiles + 1].astype(f32)
    for s in range(m):
        spread(n + m + s, tr, tl, s)

    peers(lambda p: p1(p).wait_send())

    def sent(ok, got, src, dst, c):
        @pl.when(ok)
        def _():
            c.wait_send()
    halos(sent)


def pair_kernel(
    dilation, band, near, cols, vcol, cot, halo, kf, bias,
    out, rout, cout, kgrad,
    act3, gz3, gzm, hid, der, tf, tb, kacc, bacc, rsum, csum, vbuf,
):
    n = out.shape[0]
    ch = out.shape[1]
    wide = 2 * n
    r, w, d0 = dilation[0], band[0], lax.axis_index("diag") * n
    groups = n // RG
    blk = RG * ch
    lane1 = lax.broadcasted_iota(jnp.int32, (RG, wide), 1)

    def offsets(i):
        d = lane1 - i
        d = jnp.where(d < -(n // 2), d + wide, d)
        return jnp.where(d >= wide - n // 2, d - wide, d)

    def at_row(i, first, size):
        half = jnp.where((i < 0) | (i >= n), 1, 0)
        x = pltpu.roll(near[half, first : first + size, :], lax.rem(2 * n - i, n), 1)
        return jnp.broadcast_to(x[:, :1], (size, wide))

    def validity(i, side):
        d = offsets(i)
        inside = (d + d0 >= 0) & (d + d0 < w)
        v = jnp.where(inside, vcol[side] * at_row(i, ch, RG), 0.0)
        return v, d

    def tiled(x):
        return jnp.concatenate([jnp.concatenate([x] * 4, axis=1)] * (2 * blk // (4 * ch)), axis=1)

    kblk = lax.broadcasted_iota(jnp.int32, (ch, 2 * blk), 1) // ch
    for b in range(3):
        fw = [tiled(kf[3 * a + b].astype(jnp.float32)) for a in range(3)]
        bw = [tiled(kf[3 * a + b].astype(jnp.float32).T) for a in range(3)]
        for ii in range(RG):
            f = jnp.zeros((ch, 2 * blk), jnp.float32)
            g = jnp.zeros((ch, 2 * blk), jnp.float32)
            for a in range(3):
                f = jnp.where(kblk == ii + MAXDIL + (a - 1) * r, fw[a], f)
                g = jnp.where(kblk == ii + MAXDIL - (a - 1) * r, bw[a], g)
            tf[b, ii * ch : (ii + 1) * ch, :] = f.astype(jnp.bfloat16)
            tb[b, ii * ch : (ii + 1) * ch, :] = g.astype(jnp.bfloat16)

    def phase_a(gi, carry):
        side = jnp.where(gi * RG > n // 2, 1, 0)
        for ii in range(RG):
            e = gi * RG + ii
            i = e - MAXDIL
            v8, d8 = validity(i, side)
            vbuf[e] = v8
            v = jnp.concatenate([v8] * (ch // RG), axis=0)
            d = jnp.concatenate([d8] * (ch // RG), axis=0)
            h = (at_row(i, 0, ch) + cols[side]) * v
            h2 = h * h
            t = jnp.tanh(S2PI * h * (1.0 + CUBIC * h2))
            cdf = 0.5 * (1.0 + t)
            act = h * cdf
            dg = cdf + (0.5 * S2PI) * h * (1.0 - t * t) * (1.0 + 3.0 * CUBIC * h2)
            at = pl.ds(pl.multiple_of(e * ch, ch), ch)
            act3[1, at, :] = act.astype(jnp.bfloat16)
            act3[0, at, :] = pltpu.roll(act, r, 1).astype(jnp.bfloat16)
            act3[2, at, :] = pltpu.roll(act, wide - r, 1).astype(jnp.bfloat16)
            ct = jnp.concatenate([cot[e].astype(jnp.float32), halo[e].astype(jnp.float32)], axis=1)
            gz = pltpu.roll(ct, lax.rem(i + wide, wide), 1) * v
            main = (d >= 0) & (d < n)
            gz3[1, at, :] = gz.astype(jnp.bfloat16)
            gz3[2, at, :] = pltpu.roll(gz, r, 1).astype(jnp.bfloat16)
            gz3[0, at, :] = pltpu.roll(gz, wide - r, 1).astype(jnp.bfloat16)
            gzm[at, :] = jnp.where(main, gz, 0.0).astype(jnp.bfloat16)
            hid[at, :] = h
            der[at, :] = jnp.where(main, dg * v, 0.0)
        return carry

    lax.fori_loop(0, groups + 1, phase_a, 0)

    kacc[...] = jnp.zeros_like(kacc)
    bacc[...] = jnp.zeros_like(bacc)
    rsum[...] = jnp.zeros_like(rsum)
    csum[...] = jnp.zeros_like(csum)
    lane_n = lax.broadcasted_iota(jnp.int32, (ch, n), 1)

    bias_all = jnp.broadcast_to(bias[...], (ch, wide))

    def phase_b(gi, carry):
        big = pl.ds(pl.multiple_of(gi * blk, blk), 2 * blk)
        own = pl.ds(pl.multiple_of(gi * blk + MAXDIL * ch, MAXDIL * ch), blk)
        z = jnp.zeros((blk, wide), jnp.float32)
        da = jnp.zeros((blk, wide), jnp.float32)
        g = gzm[own, :]
        for b in range(3):
            x = act3[b, big, :]
            z = z + jnp.dot(tf[b], x, preferred_element_type=jnp.float32)
            da = da + jnp.dot(tb[b], gz3[b, big, :], preferred_element_type=jnp.float32)
            kacc[b] += lax.dot_general(g, x, (((1,), (1,)), ((), ())), preferred_element_type=jnp.float32)
        gf = g.astype(jnp.float32)
        dx = gf + der[own, :] * da
        hz = hid[own, :] + z
        bsum, cs, rs = bacc[...], csum[...], rsum[...]
        for ii in range(RG):
            i = gi * RG + ii
            v = jnp.concatenate([vbuf[i + MAXDIL]] * (ch // RG), axis=0)
            sl = slice(ii * ch, (ii + 1) * ch)
            po = (hz[sl] + bias_all) * v
            out[i] = pltpu.roll(po, lax.rem(wide - i, wide), 1)[:, :n].astype(jnp.bfloat16)
            bsum = bsum + gf[sl]
            cs = cs + dx[sl]
            tot = jnp.sum(dx[sl], axis=1, keepdims=True)
            rs = jnp.where(lane_n == i, tot, rs)
        bacc[...] = bsum
        csum[...] = cs
        rsum[...] = rs
        return carry

    lax.fori_loop(0, groups, phase_b, 0)

    for z in range(ch // RG):
        rout[z] = rsum[z * RG : (z + 1) * RG, :]
        for k in range(2):
            cout[k, z] = csum[z * RG : (z + 1) * RG, k * n : (k + 1) * n]
    lanes = lax.broadcasted_iota(jnp.int32, (RG, 128), 1) // ch
    pieces = []
    for a in range(3):
        for b in range(3):
            s = jnp.zeros((ch, 2 * blk), jnp.float32)
            for ii in range(RG):
                s = s + jnp.where(kblk == ii + MAXDIL + (a - 1) * r, kacc[b, ii * ch : (ii + 1) * ch, :], 0.0)
            f = s[:, :128]
            for m in range(1, 2 * blk // 128):
                f = f + s[:, m * 128 : (m + 1) * 128]
            f = f + pltpu.roll(f, 64, 1)
            f = f + pltpu.roll(f, 32, 1)
            pieces += [f[m * RG : (m + 1) * RG] for m in range(ch // RG)]
    bt = jnp.broadcast_to(jnp.sum(bacc[...], axis=1, keepdims=True), (ch, 128))
    count = len(pieces) // 4
    for s in range(count):
        piece = pieces[s]
        for m in range(1, 4):
            piece = jnp.where(lanes == m, pieces[m * count + s], piece)
        kgrad[s] = piece
    piece = bt[:RG]
    for m in range(1, 4):
        piece = jnp.where(lanes == m, bt[m * RG : (m + 1) * RG], piece)
    kgrad[count] = piece


def sum_kernel(
    R, T, embed_scale, weight_scale, kg, row, col, kg_out, row_out, col_out,
    kbuf, rbuf, abuf, bbuf, ksum, rcsum, kres, rcres,
    ks, kr, rs, rr, as_, ar, bs, br, k2s, k2r, r2s, r2r,
):
    N = R * T
    K, Z = kg.shape[0], row.shape[0]
    q, t = lax.axis_index("row"), lax.axis_index("diag")
    me = q * T + t

    barrier = pltpu.get_barrier_semaphore()

    def greet(p):
        @pl.when(p != me)
        def _():
            pl.semaphore_signal(barrier, inc=1, device_id={"row": p // T, "diag": p % T},
                                device_id_type=pl.DeviceIdType.MESH)
    loop(N, greet)
    pl.semaphore_wait(barrier, N - 1)

    def k1(k):
        return send(kg.at[k], kbuf.at[me], ks.at[k], kr.at[me], k // T, k % T)

    def r1(z):
        return send(row.at[z], rbuf.at[t], rs.at[z], rr.at[t], q, z)

    def a1(z):
        return send(col.at[0, z], abuf.at[q], as_.at[z], ar.at[q], q + t, z)

    def b1(z):
        return send(col.at[1, z], bbuf.at[q], bs.at[z], br.at[q], q + t + 1, z)

    def first(act):
        for k in range(K):
            @pl.when(me != k)
            def _():
                act(k1(k))
        for z in range(Z):
            @pl.when(t != z)
            def _():
                act(r1(z))

            @pl.when((q + t < R) & ((t != 0) | (z != 0)))
            def _():
                act(a1(z))

            @pl.when(q + t + 1 < R)
            def _():
                act(b1(z))

    first(lambda c: c.start())

    def got(buf, sem):
        send(buf, buf, sem, sem, q, t).wait_recv()

    def k2(p):
        return send(ksum, kres.at[me], k2s.at[p], k2r.at[me], p // T, p % T)

    def r2(p):
        return send(rcsum, rcres.at[t], r2s.at[p], r2r.at[t], q, p)

    def second(act):
        @pl.when(me < K)
        def _():
            def one(p):
                @pl.when(p != me)
                def _():
                    act(k2(p))
            loop(N, one)

        @pl.when(t < Z)
        def _():
            def one(p):
                @pl.when(p != t)
                def _():
                    act(r2(p))
            loop(T, one)

    @pl.when(me < K)
    def _():
        ksum[...] = kg[me]

        def take(p):
            @pl.when(p != me)
            def _():
                got(kbuf.at[p], kr.at[p])
                ksum[...] += kbuf[p]
        loop(N, take)
        ksum[...] = ksum[...] * weight_scale
        kres[me] = ksum[...]

    @pl.when(t < Z)
    def _():
        rcsum[0] = row[t]
        rcsum[1] = jnp.zeros_like(rcsum[1])

        def take(p):
            @pl.when(p != t)
            def _():
                got(rbuf.at[p], rr.at[p])
                rcsum[0] += rbuf[p]
        loop(T, take)

        @pl.when(t == 0)
        def _():
            rcsum[1] = col[0, 0]

        def take_col(p):
            @pl.when((p <= q) & (q - p < T) & ((p != q) | (t != 0)))
            def _():
                got(abuf.at[p], ar.at[p])
                rcsum[1] += abuf[p]

            @pl.when((p <= q - 1) & (q - 1 - p < T))
            def _():
                got(bbuf.at[p], br.at[p])
                rcsum[1] += bbuf[p]
        loop(R, take_col)
        rcsum[...] = rcsum[...] * embed_scale
        rcres[t] = rcsum[...]

    second(lambda c: c.start())
    for k in range(K):
        @pl.when(me != k)
        def _():
            got(kres.at[k], k2r.at[k])
    for z in range(Z):
        @pl.when(t != z)
        def _():
            got(rcres.at[z], r2r.at[z])
    kg_out[...] = kres[...]
    for z in range(Z):
        row_out[z * RG : (z + 1) * RG, :] = rcres[z, 0]
        col_out[z * RG : (z + 1) * RG, :] = rcres[z, 1]
    first(lambda c: c.wait_send())
    second(lambda c: c.wait_send())


def local(emb_rows, emb_cols, kernel, bias, cotangent, valid, dilation, band):
    ch, n = emb_rows.shape
    R, T = lax.axis_size("row"), lax.axis_size("diag")
    wide, ext, m = 2 * n, n + 2 * MAXDIL, MAXDIL
    bf, f32 = jnp.bfloat16, jnp.float32

    pack = jnp.concatenate(
        [emb_cols, emb_rows, jnp.broadcast_to(valid.astype(bf)[None], (16, n))], axis=0)
    cot = jnp.transpose(cotangent, (1, 0, 2))
    vmem = pl.BlockSpec(memory_space=pltpu.VMEM)
    smem = pl.BlockSpec(memory_space=pltpu.SMEM)
    dma = pltpu.SemaphoreType.DMA
    tiles = 2 * m
    edges = lambda k: pltpu.VMEM((k, ch, n), bf)
    cols, vcol, near, cot, halo = pl.pallas_call(
        functools.partial(gather_kernel, R, T),
        out_shape=(
            jax.ShapeDtypeStruct((2, ch, wide), f32),
            jax.ShapeDtypeStruct((2, RG, wide), f32),
            jax.ShapeDtypeStruct((2, ch + RG, n), f32),
            jax.ShapeDtypeStruct((ext, ch, n), bf),
            jax.ShapeDtypeStruct((ext, ch, n), bf),
        ),
        in_specs=[vmem] * 2,
        out_specs=(vmem,) * 5,
        scratch_shapes=[
            pltpu.VMEM((R + T + 3,) + pack.shape, bf),
            edges(tiles), edges(tiles), edges(tiles + 2), edges(tiles + 2), edges(m), edges(m),
            dma((R,)), dma((R,)), dma((8,)), dma((8,)),
        ],
        compiler_params=pltpu.CompilerParams(collective_id=1, has_side_effects=True),
        name="gather_kernel",
    )(pack, cot)

    blk = RG * ch
    kf = kernel.reshape(9, ch, ch)
    bias2 = bias[:, None]
    nk = (9 * ch * ch) // (RG * 128) + 1
    Z = ch // RG
    out, rsum, csum, kg = pl.pallas_call(
        pair_kernel,
        out_shape=(
            jax.ShapeDtypeStruct((n, ch, n), bf),
            jax.ShapeDtypeStruct((Z, RG, n), f32),
            jax.ShapeDtypeStruct((2, Z, RG, n), f32),
            jax.ShapeDtypeStruct((nk, RG, 128), f32),
        ),
        in_specs=[smem, smem] + [vmem] * 7,
        out_specs=(vmem,) * 4,
        scratch_shapes=[
            pltpu.VMEM((3, ext * ch, wide), bf),
            pltpu.VMEM((3, ext * ch, wide), bf),
            pltpu.VMEM((ext * ch, wide), bf),
            pltpu.VMEM((ext * ch, wide), f32),
            pltpu.VMEM((ext * ch, wide), f32),
            pltpu.VMEM((3, blk, 2 * blk), bf),
            pltpu.VMEM((3, blk, 2 * blk), bf),
            pltpu.VMEM((3, blk, 2 * blk), f32),
            pltpu.VMEM((ch, wide), f32),
            pltpu.VMEM((ch, n), f32),
            pltpu.VMEM((ch, wide), f32),
            pltpu.VMEM((ext, RG, wide), f32),
        ],
        compiler_params=pltpu.CompilerParams(vmem_limit_bytes=56 * 2**20),
        name="pair_kernel",
    )(dilation, band, near, cols, vcol, cot, halo, kf, bias2)

    tile = lambda *lead: pltpu.VMEM(lead + (RG, n), f32)
    embed_scale = float(T * n) ** -0.5
    weight_scale = float(R * n * T * n) ** -0.5
    kg, row_grad, col_grad = pl.pallas_call(
        functools.partial(sum_kernel, R, T, embed_scale, weight_scale),
        out_shape=(
            jax.ShapeDtypeStruct((nk, RG, 128), f32),
            jax.ShapeDtypeStruct((ch, n), f32),
            jax.ShapeDtypeStruct((ch, n), f32),
        ),
        in_specs=[vmem] * 3,
        out_specs=(vmem,) * 3,
        scratch_shapes=[
            tile(R * T), tile(T), tile(R), tile(R), tile(), tile(2), tile(nk), tile(Z, 2),
            dma((nk,)), dma((R * T,)), dma((Z,)), dma((T,)), dma((Z,)), dma((R,)), dma((Z,)), dma((R,)),
            dma((R * T,)), dma((nk,)), dma((T,)), dma((Z,)),
        ],
        compiler_params=pltpu.CompilerParams(collective_id=0, has_side_effects=True),
        name="sum_kernel",
    )(kg, rsum, csum)

    kgt = kg[:-1].reshape(-1, 4, ch).transpose(1, 0, 2).reshape(3, 3, ch, ch)
    bgt = kg[-1].reshape(RG, 4, ch)[:, :, 0].T.reshape(ch)
    return (
        jnp.transpose(out, (1, 0, 2)),
        row_grad,
        col_grad,
        kgt,
        bgt,
    )


def solution(mesh):
    in_specs = (
        P(None, ("grp", "row")),
        P(None, ("grp", "row")),
        P(),
        P(),
        P(None, ("grp", "row"), "diag"),
        P(("grp", "row")),
        P("grp"),
        P("grp"),
    )
    out_specs = (
        P(None, ("grp", "row"), "diag"),
        P(None, ("grp", "row")),
        P(None, ("grp", "row")),
        P("grp", None, None, None),
        P("grp"),
    )
    return jax.shard_map(local, mesh=mesh, in_specs=in_specs, out_specs=out_specs, check_vma=False)
```

profile of v0, /device:TPU:0, one launch (start us, length us, event | category | flops | bytes accessed | tf_op | source)
XLA Modules:
  0.0 79.2 jit_solution(4560908808646368405)
XLA Ops:
  1.9 0.7 convert_element_type.3
  2.6 1.3 %pad_maximum_fusion.pack = bf16[80,128]{1,0:T(8,128)(2,1)} fusion(bf16[16,128]{1,0:T(8,128)(2,1)S(1)} %broadcast_in_dim.4, bf16[32,128]{1,0:T(8,128)(2,1)} %param.8, bf16[32,128]{1,0:T(8,128)(2,1)} %param.9), kind=kLoop, calls=%fused_computation.1 | loop fusion | flops 61440 | bytes 40960 | tf_op jit(solution)/shard_map/concatenate | solution.py:470
  3.9 1.3 %copy.23.bias = f32[32,1]{1,0:T(8,128)} copy(f32[32,1]{0,1:T(1,128)} %bitcast.19) | data formatting | bytes 256 | tf_op jit(solution)/shard_map/broadcast_in_dim | solution.py:500
  5.3 2.9 %copy.32 = bf16[32,128,128]{2,0,1:T(8,128)(2,1)} copy(bf16[32,128,128]{2,1,0:T(8,128)(2,1)} %param.12) | data formatting | bytes 2097152 | tf_op args[4]
  8.1 11.9 %gather_kernel.1 = (f32[2,32,256]{2,1,0:T(8,128)}, f32[2,8,256]{2,1,0:T(8,128)}, f32[2,40,128]{2,1,0:T(8,128)}, bf16[136,32,128]{2,1,0:T(8,128)(2,1)}, bf16[136,32,128]{2,1,0:T(8,128)(2,1)}) custom-call(bf16[80,128]{1,0:T(8,128)(2,1)} %pad_maximum_fusion.pack, bf16[128,32,128]{2,1,0:T(8,128)(2,1)} %bitcast.12), custom_call_target="tpu_custom_call" | custom-call | tf_op jit(solution)/shard_map/gather_kernel/pallas_call | solution.py:478
  20.1 36.6 %pair_kernel.1 = (bf16[128,32,128]{2,1,0:T(8,128)(2,1)}, f32[4,8,128]{2,1,0:T(8,128)}, f32[2,4,8,128]{3,2,1,0:T(8,128)}, f32[10,8,128]{2,1,0:T(8,128)}) custom-call(s32[1]{0:T(128)S(6)} %copy.35.dilation, s32[1]{0:T(128)S(6)} %copy.36.band, f32[2,40,128]{2,1,0:T(8,128)} %get-tuple-element.17.near, f32[2,32,256]{2,1,0:T(8,128)} %get-tuple-element.18.cols, ...), custom_call_target="tpu_custom_call" | custom-call | tf_op jit(solution)/shard_map/pair_kernel/pallas_call | solution.py:503
  56.7 2.6 %copy.26 = bf16[32,128,128]{2,1,0:T(8,128)(2,1)} copy(bf16[32,128,128]{2,0,1:T(8,128)(2,1)} %bitcast.13) | data formatting | bytes 2097152
  59.3 14.2 %sum_kernel.1 = (f32[10,8,128]{2,1,0:T(8,128)}, f32[32,128]{1,0:T(8,128)}, f32[32,128]{1,0:T(8,128)}) custom-call(f32[10,8,128]{2,1,0:T(8,128)} %get-tuple-element.23.kg, f32[4,8,128]{2,1,0:T(8,128)} %get-tuple-element.24.row, f32[2,4,8,128]{3,2,1,0:T(8,128)} %get-tuple-element.25.col), custom_call_target="tpu_custom_call" | custom-call | tf_op jit(solution)/shard_map/sum_kernel/pallas_call | solution.py:534
  73.5 0.7 slice.10
  74.2 0.8 slice.9
  75.0 0.1 reshape_squeeze.3
  75.0 0.1 copy.30
  75.1 0.6 reshape.26
  75.7 0.1 reshape.24
  75.9 0.7 copy.28
  76.5 1.3 %copy.37 = f32[32,128]{1,0:T(8,128)} copy(f32[32,128]{1,0:T(8,128)} %get-tuple-element.50) | data formatting | bytes 32768
  77.9 1.3 %copy.38 = f32[32,128]{1,0:T(8,128)} copy(f32[32,128]{1,0:T(8,128)} %get-tuple-element.51) | data formatting | bytes 32768
  (1 shorter events, 0.0 us)
where the time goes:
time: 79.8 us; the launch traced here: 79.2 us
  Pallas kernels  62.8 us (79%)
  local copies, waits for them, and re-layouts  12.5 us (16%)
  other arithmetic  1.98 us (2%)
  between operations  1.96 us (2%)
    pallas_call x1, Pallas kernels, local(): pl.pallas_call(pair_kernel, out_shape=(jax.ShapeDtypeStruct((n, ch, n), b...  36.6 us
    pallas_call x1, Pallas kernels, local(): pl.pallas_call(functools.partial(sum_kernel, R, T, embed_scale, weight_sc...  14.2 us
    pallas_call x1, Pallas kernels, local(): pl.pallas_call(functools.partial(gather_kernel, R, T), out_shape=(jax.Sha...  11.9 us
    unnamed x6, local copies, waits for them, and re-layouts  8.9 us

commit v1 on v0

v1 whole, which is shorter than its diff:
```python
import functools

import jax
import jax.numpy as jnp
from jax import lax
from jax.experimental import pallas as pl
from jax.experimental.pallas import tpu as pltpu
from jax.sharding import PartitionSpec as P

MAXDIL = 4
RG = 8
S2PI = 0.7978845608028654
CUBIC = 0.044715
bf, f32 = jnp.bfloat16, jnp.float32


def loop(count, body):
    def step(p, c):
        body(p)
        return c
    lax.fori_loop(0, count, step, 0)


def send(src, dst, ss, sr, dq, dt):
    return pltpu.make_async_remote_copy(
        src_ref=src, dst_ref=dst, send_sem=ss, recv_sem=sr,
        device_id={"row": dq, "diag": dt}, device_id_type=pl.DeviceIdType.MESH,
    )


def gelu_parts(h):
    h2 = h * h
    t = jnp.tanh(h * (S2PI + (S2PI * CUBIC) * h2))
    cdf = 0.5 + 0.5 * t
    return h2, t, cdf


def divisor(total, limit):
    return max(k for k in range(1, limit + 1) if total % k == 0)


def fused_kernel(
    R, T, embed_scale, weight_scale,
    dilation, band, rows, cols, valid, kf, bias, cot,
    out, kres, rcres,
    pack, blocks, cf, ct, edge_l, edge_r, from_r, from_l,
    cw, nr, hlc, hlr, hact, hval,
    act5, gz5, gzm, hid, der, vb, vb16, yz, yd, wz, wd, kacc, bacc, kg, row, col,
    kbuf, rbuf, abuf, bbuf, ksum, rcsum,
    ps, pr, hs, hr, ks, kr, rs, rr, as_, ar, bs, br, k2s, k2r, r2s, r2r,
):
    ch, n = rows.shape
    m = MAXDIL
    width = 2 * m
    per = n // width
    tiles = n // per
    ext = n + 2 * m
    stride = cf.shape[0] // ch
    N = R * T
    K, Z = kg.shape[0], row.shape[0]
    q, t = lax.axis_index("row"), lax.axis_index("diag")
    me = q * T + t
    r, w = dilation[0], band[0]
    mesh_id = pl.DeviceIdType.MESH
    barrier = pltpu.get_barrier_semaphore()
    left, right, above, below = t > 0, t < T - 1, q > 0, q < R - 1

    def greet(p):
        @pl.when(p != me)
        def _():
            pl.semaphore_signal(barrier, inc=1, device_id={"row": p // T, "diag": p % T}, device_id_type=mesh_id)
    loop(N, greet)

    pack[0:ch] = cols[...]
    pack[ch : 2 * ch] = rows[...]
    pack[2 * ch : 2 * ch + 16] = jnp.broadcast_to(valid[...].astype(f32), (16, n)).astype(bf)
    zero = jnp.zeros(pack.shape, bf)
    blocks[0] = zero
    for k in range(R + 1, R + T + 3):
        blocks[k] = zero
    blocks[q + 1] = pack[...]
    pl.semaphore_wait(barrier, N - 1)

    def p1(p):
        return send(pack, blocks.at[q + 1], ps.at[p], pr.at[q], p, t)

    def peers(act):
        def one(p):
            @pl.when(p != q)
            def _():
                act(p)
        loop(R, one)
    peers(lambda p: p1(p).start())

    lane = lax.broadcasted_iota(jnp.int32, (ch, n), 1)

    def spread(c):
        cf[pl.ds(pl.multiple_of(c * stride, 8), n), :] = cot[c].astype(f32)
    loop(ch, spread)

    def pack_edges(g):
        a = jnp.zeros((ch, n), bf)
        b = jnp.zeros((ch, n), bf)
        for s in range(per):
            i = g * per + s
            x = cf[pl.ds(i, ch, stride=stride), :].astype(bf)
            ct[m + i] = x
            here = lane // width == s
            a = jnp.where(here, pltpu.roll(x, width * s, 1) if s else x, a)
            sh = (width * (s + 1)) % n
            b = jnp.where(here, pltpu.roll(x, sh, 1) if sh else x, b)
        edge_l[g] = a
        edge_r[g] = b
    loop(tiles, pack_edges)

    def halos(act):
        last = tiles - 1
        plan = (
            (left, edge_l, from_r.at[pl.ds(1, tiles)], 0, 0, -1),
            (right, edge_r, from_l.at[pl.ds(1, tiles)], 1, 0, 1),
            (above, ct.at[pl.ds(m, m)], ct.at[pl.ds(n + m, m)], 2, -1, 0),
            (below, ct.at[pl.ds(n, m)], ct.at[pl.ds(0, m)], 3, 1, 0),
            (below & left, edge_l.at[last], from_r.at[0], 4, 1, -1),
            (above & left, edge_l.at[0], from_r.at[tiles + 1], 5, -1, -1),
            (below & right, edge_r.at[last], from_l.at[0], 6, 1, 1),
            (above & right, edge_r.at[0], from_l.at[tiles + 1], 7, -1, 1),
        )
        flags = {(0, -1): right, (0, 1): left, (-1, 0): below, (1, 0): above,
                 (1, -1): above & right, (-1, -1): below & right, (1, 1): above & left, (-1, 1): below & left}
        for ok, src, dst, k, dq, dt in plan:
            act(ok, flags[(dq, dt)], src, dst, send(src, dst, hs.at[k], hr.at[k], q + dq, t + dt))

    def start(ok, got, src, dst, c):
        @pl.when(ok)
        def _():
            c.start()
    halos(start)

    for a in range(3):
        zrow, drow = [None] * 5, [None] * 5
        for b in range(3):
            x = kf[3 * a + b].astype(f32)
            zrow[b - a + 2] = x
            drow[a - b + 2] = x.T
        blank = jnp.zeros((ch, ch), f32)
        fill = lambda xs: jnp.concatenate([blank if x is None else x for x in xs], axis=1).astype(bf)
        wz[a * ch : (a + 1) * ch, :] = fill(zrow)
        wd[a * ch : (a + 1) * ch, :] = fill(drow)

    peers(lambda p: send(pack, blocks.at[p + 1], ps.at[p], pr.at[p], q, t).wait_recv())

    d0 = t * n
    v0 = 2 * ch
    for k in range(4):
        x = blocks[q + t + k].astype(f32)
        cw[k, 0:ch] = x[0:ch]
        cw[k, ch : ch + RG] = x[v0 : v0 + RG]
    for k in range(3):
        x = blocks[q + k].astype(f32)
        nr[k, 0:ch] = x[ch : 2 * ch]
        nr[k, ch : ch + RG] = x[v0 : v0 + RG]

    hrows = ch + 16
    slots = tiles + 2
    lane_h = lax.broadcasted_iota(jnp.int32, (hrows, n), 1)
    cblk = [jnp.concatenate([blocks[q + t + k, 0:ch], blocks[q + t + k, v0 : v0 + 16]], axis=0) for k in range(4)]
    rblk = [jnp.concatenate([blocks[q + k, ch : 2 * ch], blocks[q + k, v0 : v0 + 16]], axis=0) for k in range(3)]

    def window(blks, base):
        k, sh = base // n, base % n
        x = blks[k]
        if sh:
            if k + 1 < len(blks):
                x = jnp.where(lane_h >= sh, x, blks[k + 1])
            x = pltpu.roll(x, n - sh, 1)
        return x
    for g in range(slots):
        for side, off in ((0, 2 * n - per), (1, n - per - width)):
            hlc[(2 * g + side) * hrows : (2 * g + side + 1) * hrows, :] = window(cblk, per * g + off)
        hlr[g * hrows : (g + 1) * hrows, :] = window(rblk, per * g + n - per)
    src = lax.broadcasted_iota(jnp.int32, (n, n), 0)
    dst = lax.broadcasted_iota(jnp.int32, (n, n), 1)
    one = lambda cond: jnp.where(cond, 1.0, 0.0).astype(bf)
    hc = jnp.dot(hlc[...], one(src == dst // width + dst % width), preferred_element_type=f32)
    hw = jnp.dot(hlr[...], one(src == dst // width), preferred_element_type=f32)
    kk = lax.broadcasted_iota(jnp.int32, (RG, n), 1) % width
    for g in range(slots):
        hrw = hw[g * hrows : (g + 1) * hrows]
        for side in range(2):
            hcc = hc[(2 * g + side) * hrows : (2 * g + side + 1) * hrows]
            da = d0 + kk + (-width if side else n)
            v8 = jnp.where((da >= 0) & (da < w), hcc[ch : ch + RG] * hrw[ch : ch + RG], 0.0)
            v = jnp.concatenate([v8] * (ch // RG), axis=0)
            h = (hrw[0:ch] + hcc[0:ch]) * v
            _, _, cdf = gelu_parts(h)
            hact[side, g] = (h * cdf).astype(bf)
            hval[side, g] = jnp.concatenate([v8, v8], axis=0).astype(bf)

    lane8 = lax.broadcasted_iota(jnp.int32, (RG, n), 1)
    lane40 = lax.broadcasted_iota(jnp.int32, (ch + RG, n), 1)

    def shifts(dst, e, main, hright, hleft):
        s = lax.rem(e + per - m, per)
        a = pltpu.roll(hright, lax.rem(n - width * s, n), 1)
        b = pltpu.roll(hleft, lax.rem(2 * n - width - width * s, n), 1)
        hx = jnp.where(lane < n // 2, a, b)
        dst[e, 2 * ch : 3 * ch] = main
        for k in (1, 2):
            sr = k * r
            dst[e, (2 + k) * ch : (3 + k) * ch] = pltpu.roll(jnp.where(lane < sr, hx, main), n - sr, 1)
            dst[e, (2 - k) * ch : (3 - k) * ch] = pltpu.roll(jnp.where(lane >= n - sr, hx, main), sr, 1)

    def phase_a1(gi):
        for ii in range(RG):
            e = gi * RG + ii
            at = e - m + n
            k, sh = at // n, lax.rem(at, n)
            c = pltpu.roll(jnp.where(lane40 >= sh, cw[k], cw[k + 1]), lax.rem(n - sh, n), 1)
            rw = jnp.take_along_axis(nr[k], jnp.full((ch + RG, n), sh, jnp.int32), axis=1)
            v8 = jnp.where(lane8 + d0 < w, c[ch:] * rw[ch:], 0.0)
            vb[e] = v8
            vb16[e] = jnp.concatenate([v8, v8], axis=0).astype(bf)
            v = jnp.concatenate([v8] * (ch // RG), axis=0)
            h = (rw[:ch] + c[:ch]) * v
            h2, tt, cdf = gelu_parts(h)
            hid[e] = h
            der[e] = (cdf + (0.5 * h) * (1.0 - tt * tt) * (S2PI + (3.0 * CUBIC * S2PI) * h2)) * v
            slot = (e + per - m) // per
            shifts(act5, e, (h * cdf).astype(bf), hact[0, slot], hact[1, slot])
    loop(ext // RG, phase_a1)

    def finish(ok, got, src, dst, c):
        @pl.when(got)
        def _():
            c.wait_recv()

        @pl.when(jnp.logical_not(got))
        def _():
            dst[...] = jnp.zeros(dst.shape, bf)
    halos(finish)

    def halo_gz(g):
        for side, buf in ((0, from_r), (1, from_l)):
            x = hval[side, g]
            buf[g] = buf[g] * jnp.concatenate([x, x], axis=0)
    loop(slots, halo_gz)
    bacc[...] = jnp.zeros_like(bacc)
    for e in range(2 * m):
        gzm[e] = jnp.zeros((ch, n), bf)
        gzm[n + 2 * m + e] = jnp.zeros((ch, n), bf)

    def gz_row(e, inner):
        x = vb16[e]
        g = ct[e] * jnp.concatenate([x, x], axis=0)
        slot = (e + per - m) // per
        shifts(gz5, e, g, from_r[slot], from_l[slot])
        if inner:
            gzm[e + m] = g
            return g.astype(f32)

    def phase_a2(gi):
        tot = bacc[...]
        for ii in range(RG):
            tot = tot + gz_row(m + gi * RG + ii, True)
        bacc[...] = tot
    loop(n // RG, phase_a2)

    def outer_rows(s):
        gz_row(s, False)
        gz_row(n + m + s, False)
    loop(m, outer_rows)

    gr = divisor(ext, 34)
    kacc[...] = jnp.zeros_like(kacc)

    def phase_k(gi):
        xs, gs, ys = [], [], []
        for ii in range(gr):
            e = gi * gr + ii
            xs.append(act5[e])
            ys.append(gz5[e])
            gs.append(jnp.concatenate([gzm[e + m - (a - 1) * r] for a in range(3)], axis=0))
        kacc[...] += lax.dot_general(jnp.concatenate(gs, axis=1), jnp.concatenate(xs, axis=1),
                                     (((1,), (1,)), ((), ())), preferred_element_type=f32)
        y = jnp.dot(wd[...], jnp.concatenate(ys, axis=1), preferred_element_type=f32)
        for ii in range(gr):
            yd[gi * gr + ii] = y[:, ii * n : (ii + 1) * n]
    loop(ext // gr, phase_k)

    for a in range(3):
        for b in range(3):
            k = b - a + 2
            x = kacc[a * ch : (a + 1) * ch, k * ch : (k + 1) * ch]
            kg[3 * a + b] = jnp.concatenate([x[z * RG : (z + 1) * RG] for z in range(ch // RG)], axis=1)
    diag = lax.broadcasted_iota(jnp.int32, (ch, n), 0) == lane
    bt = jnp.sum(bacc[...], axis=1, keepdims=True)
    kg[9] = jnp.broadcast_to(jnp.sum(jnp.where(diag, bt, 0.0), axis=0, keepdims=True), (RG, n))

    def phase_b(gi, carry):
        lo, hi, rsum = carry
        for ii in range(RG):
            i = gi * RG + ii
            da = yd[m + i + r, 0:ch] + yd[m + i, ch : 2 * ch] + yd[m + i - r, 2 * ch : 3 * ch]
            dx = gzm[i + 2 * m].astype(f32) + der[m + i] * da
            x = pltpu.roll(dx, i, 1)
            wrap = lane < i
            lo = lo + jnp.where(wrap, 0.0, x)
            hi = hi + jnp.where(wrap, x, 0.0)
            rsum = jnp.where(lane == i, jnp.sum(dx, axis=1, keepdims=True), rsum)
        return lo, hi, rsum
    zf = jnp.zeros((ch, n), f32)
    lo, hi, rsum = lax.fori_loop(0, n // RG, phase_b, (zf, zf, zf))
    for z in range(Z):
        sl = slice(z * RG, (z + 1) * RG)
        row[z] = rsum[sl]
        col[0, z] = lo[sl]
        col[1, z] = hi[sl]

    def k1(k):
        return send(kg.at[k], kbuf.at[me], ks.at[k], kr.at[me], k // T, k % T)

    def r1(z):
        return send(row.at[z], rbuf.at[t], rs.at[z], rr.at[t], q, z)

    def a1(z):
        return send(col.at[0, z], abuf.at[q], as_.at[z], ar.at[q], q + t, z)

    def b1(z):
        return send(col.at[1, z], bbuf.at[q], bs.at[z], br.at[q], q + t + 1, z)

    def first(act):
        for k in range(K):
            @pl.when(me != k)
            def _():
                act(k1(k))
        for z in range(Z):
            @pl.when(t != z)
            def _():
                act(r1(z))

            @pl.when((q + t < R) & ((t != 0) | (z != 0)))
            def _():
                act(a1(z))

            @pl.when(q + t + 1 < R)
            def _():
                act(b1(z))

    first(lambda c: c.start())

    def phase_z(gi):
        x = jnp.concatenate([act5[gi * gr + ii] for ii in range(gr)], axis=1)
        y = jnp.dot(wz[...], x, preferred_element_type=f32)
        for ii in range(gr):
            yz[gi * gr + ii] = y[:, ii * n : (ii + 1) * n]
    loop(ext // gr, phase_z)
    eye = lax.broadcasted_iota(jnp.int32, (ch, ch), 0) == lax.broadcasted_iota(jnp.int32, (ch, ch), 1)
    bcol = jnp.sum(jnp.where(eye, bias[...], 0.0), axis=1, keepdims=True)
    bias_all = jnp.broadcast_to(bcol, (ch, n))

    def phase_o(gi):
        for ii in range(RG):
            i = gi * RG + ii
            z = yz[m + i - r, 0:ch] + yz[m + i, ch : 2 * ch] + yz[m + i + r, 2 * ch : 3 * ch]
            v = jnp.concatenate([vb[m + i]] * (ch // RG), axis=0)
            cf[pl.ds(i, ch, stride=stride), :] = (hid[m + i] + z + bias_all) * v
    loop(n // RG, phase_o)

    def emit(c):
        out[c] = cf[pl.ds(pl.multiple_of(c * stride, 8), n), :].astype(bf)
    loop(ch, emit)

    def got(buf, sem):
        send(buf, buf, sem, sem, q, t).wait_recv()

    def k2(p):
        return send(ksum, kres.at[me], k2s.at[p], k2r.at[me], p // T, p % T)

    def r2(p):
        return send(rcsum, rcres.at[t], r2s.at[p], r2r.at[t], q, p)

    def second(act):
        @pl.when(me < K)
        def _():
            def one(p):
                @pl.when(p != me)
                def _():
                    act(k2(p))
            loop(N, one)

        @pl.when(t < Z)
        def _():
            def one(p):
                @pl.when(p != t)
                def _():
                    act(r2(p))
            loop(T, one)

    @pl.when(me < K)
    def _():
        ksum[...] = kg[me]

        def take(p):
            @pl.when(p != me)
            def _():
                got(kbuf.at[p], kr.at[p])
                ksum[...] += kbuf[p]
        loop(N, take)
        ksum[...] = ksum[...] * weight_scale
        kres[me] = ksum[...]

    @pl.when(t < Z)
    def _():
        rcsum[0] = row[t]
        rcsum[1] = jnp.zeros_like(rcsum[1])

        def take(p):
            @pl.when(p != t)
            def _():
                got(rbuf.at[p], rr.at[p])
                rcsum[0] += rbuf[p]
        loop(T, take)

        @pl.when(t == 0)
        def _():
            rcsum[1] = col[0, 0]

        def take_col(p):
            @pl.when((p <= q) & (q - p < T) & ((p != q) | (t != 0)))
            def _():
                got(abuf.at[p], ar.at[p])
                rcsum[1] += abuf[p]

            @pl.when((p <= q - 1) & (q - 1 - p < T))
            def _():
                got(bbuf.at[p], br.at[p])
                rcsum[1] += bbuf[p]
        loop(R, take_col)
        rcsum[...] = rcsum[...] * embed_scale
        rcres[t] = rcsum[...]

    second(lambda c: c.start())
    for k in range(K):
        @pl.when(me != k)
        def _():
            got(kres.at[k], k2r.at[k])
    for z in range(Z):
        @pl.when(t != z)
        def _():
            got(rcres.at[z], r2r.at[z])
    peers(lambda p: p1(p).wait_send())

    def sent(ok, got, src, dst, c):
        @pl.when(ok)
        def _():
            c.wait_send()
    halos(sent)
    first(lambda c: c.wait_send())
    second(lambda c: c.wait_send())


def finish_kernel(pair, kres, rcres, out, row_out, col_out, kg_out, bg_out):
    out[...] = pair[...]
    ch = row_out.shape[0]
    for z in range(ch // RG):
        row_out[z * RG : (z + 1) * RG, :] = rcres[z, 0]
        col_out[z * RG : (z + 1) * RG, :] = rcres[z, 1]
        for s in range(9):
            kg_out[s, z * RG : (z + 1) * RG, :] = kres[s, :, z * ch : (z + 1) * ch]
    bg_out[...] = kres[9, 0:1, 0:ch]


def local(emb_rows, emb_cols, kernel, bias, cotangent, valid, dilation, band):
    ch, n = emb_rows.shape
    R, T = lax.axis_size("row"), lax.axis_size("diag")
    m = MAXDIL
    ext = n + 2 * m
    vmem = pl.BlockSpec(memory_space=pltpu.VMEM)
    smem = pl.BlockSpec(memory_space=pltpu.SMEM)
    dma = pltpu.SemaphoreType.DMA
    V = pltpu.VMEM
    width = 2 * m
    per = n // width
    tiles = n // per
    slots = tiles + 2
    hrows = ch + 16
    kf = kernel.reshape(9, ch, ch)
    nk = (9 * ch * ch) // (RG * 128) + 1
    Z = ch // RG
    tile = lambda *lead: V(lead + (RG, n), f32)
    edges = lambda k: V((k, ch, n), bf)
    embed_scale = float(T * n) ** -0.5
    weight_scale = float(R * n * T * n) ** -0.5
    pair, kres, rcres = pl.pallas_call(
        functools.partial(fused_kernel, R, T, embed_scale, weight_scale),
        out_shape=(
            jax.ShapeDtypeStruct((ch, n, n), bf),
            jax.ShapeDtypeStruct((nk, RG, n), f32),
            jax.ShapeDtypeStruct((Z, 2, RG, n), f32),
        ),
        in_specs=[smem, smem] + [vmem] * 6,
        out_specs=(vmem,) * 3,
        scratch_shapes=[
            V((2 * ch + 16, n), bf), V((R + T + 3, 2 * ch + 16, n), bf), V((ch * (n + 8), n), f32),
            edges(ext), edges(tiles), edges(tiles), edges(slots), edges(slots),
            V((4, ch + RG, n), f32), V((3, ch + RG, n), f32),
            V((slots * 2 * hrows, n), bf), V((slots * hrows, n), bf),
            V((2, slots, ch, n), bf), V((2, slots, 16, n), bf),
            V((ext, 5 * ch, n), bf), V((ext, 5 * ch, n), bf), V((ext + 2 * m, ch, n), bf),
            V((ext, ch, n), f32), V((ext, ch, n), f32), V((ext, RG, n), f32), V((ext, 16, n), bf),
            V((ext, 3 * ch, n), f32), V((ext, 3 * ch, n), f32),
            V((3 * ch, 5 * ch), bf), V((3 * ch, 5 * ch), bf), V((3 * ch, 5 * ch), f32),
            V((ch, n), f32), tile(nk), tile(Z), tile(2, Z),
            tile(R * T), tile(T), tile(R), tile(R), tile(), tile(2),
            dma((R,)), dma((R,)), dma((8,)), dma((8,)),
            dma((nk,)), dma((R * T,)), dma((Z,)), dma((T,)), dma((Z,)), dma((R,)), dma((Z,)), dma((R,)),
            dma((R * T,)), dma((nk,)), dma((T,)), dma((Z,)),
        ],
        compiler_params=pltpu.CompilerParams(collective_id=0, has_side_effects=True, vmem_limit_bytes=56 * 2**20),
        name="fused_kernel",
    )(dilation, band, emb_rows, emb_cols, valid[None, :], kf, bias[None, :], cotangent)

    out, row_grad, col_grad, kgt, bgt = pl.pallas_call(
        finish_kernel,
        out_shape=(
            jax.ShapeDtypeStruct((ch, n, n), bf),
            jax.ShapeDtypeStruct((ch, n), f32),
            jax.ShapeDtypeStruct((ch, n), f32),
            jax.ShapeDtypeStruct((9, ch, ch), f32),
            jax.ShapeDtypeStruct((1, ch), f32),
        ),
        in_specs=[vmem] * 3,
        out_specs=(vmem,) * 5,
        name="finish_kernel",
    )(pair, kres, rcres)
    return out, row_grad, col_grad, kgt.reshape(3, 3, ch, ch), bgt.reshape(ch)


def solution(mesh):
    in_specs = (
        P(None, ("grp", "row")),
        P(None, ("grp", "row")),
        P(),
        P(),
        P(None, ("grp", "row"), "diag"),
        P(("grp", "row")),
        P("grp"),
        P("grp"),
    )
    out_specs = (
        P(None, ("grp", "row"), "diag"),
        P(None, ("grp", "row")),
        P(None, ("grp", "row")),
        P("grp", None, None, None),
        P("grp"),
    )
    return jax.shard_map(local, mesh=mesh, in_specs=in_specs, out_specs=out_specs, check_vma=False)
```

time: 79.8 us -> 46.6 us (0.58)
  Pallas kernels: 62.8 us -> 44.4 us
  local copies, waits for them, and re-layouts: 12.5 us -> 0 us
  other arithmetic: 1.98 us -> 0 us
    pallas_call x3 -> x2, Pallas kernels: 62.8 us -> 44.4 us  [the longest x1 42.1 us: local(): pl.pallas_call(functools.partial(fused_kernel, R, T, embed_scale, weight_...]
    unnamed x6 -> x0, local copies, waits for them, and re-layouts: 8.9 us -> none
    slice x2 -> x0, local copies, waits for them, and re-layouts: 1.46 us -> none  [the longest x1 0.77 us: local(): kgt = kg[:-1].reshape(-1, 4, ch).transpose(1, 0, 2).reshape(3, 3, ch, ch)]
    broadcast_in_dim x2 -> x0, local copies, waits for them, and re-layouts: 1.35 us -> none  [the longest x1 1.34 us: local(): bias2 = bias[:, None]]
    concatenate x1 -> x0, other arithmetic: 1.32 us -> none  [local(): jnp.concatenate([emb_cols, emb_rows, jnp.broadcast_to(valid.astype(bf)[No...]
where the time goes in v1:
time: 46.6 us; the launch traced here: 46.4 us
  Pallas kernels  44.4 us (95%)
  between operations  1.93 us (4%)
    pallas_call x1, Pallas kernels, local(): pl.pallas_call(functools.partial(fused_kernel, R, T, embed_scale, weight_...  42.1 us
    pallas_call x1, Pallas kernels, local(): pl.pallas_call(finish_kernel, out_shape=(jax.ShapeDtypeStruct((ch, n, n),...  2.34 us

profile of v1, /device:TPU:0, one launch (start us, length us, event | category | flops | bytes accessed | tf_op | source)
XLA Modules:
  0.0 46.4 jit_solution(17642030995153193264)
XLA Ops:
  1.9 42.1 %fused_kernel.1 = (bf16[32,128,128]{2,1,0:T(8,128)(2,1)}, f32[10,8,128]{2,1,0:T(8,128)}, f32[4,2,8,128]{3,2,1,0:T(8,128)}) custom-call(s32[1]{0:T(128)S(6)} %copy.13.dilation, s32[1]{0:T(128)S(6)} %copy.14.band, bf16[32,128]{1,0:T(8,128)(2,1)} %rows.1, bf16[32,128]{1,0:T(8,128)(2,1)} %cols.1, s32[1,128]{1,0:T(1,128)} %bitcast.6, bf16[9,32,32]{2,1,0:T(8,128)(2,1)} %bitcast.5, ...), custom_call_target="tpu_custom_call" | custom-call | tf_op jit(solution)/shard_map/fused_kernel/pallas_call | solution.py:494
  44.0 2.3 %finish_kernel.1 = (bf16[32,128,128]{2,1,0:T(8,128)(2,1)}, f32[32,128]{1,0:T(8,128)}, f32[32,128]{1,0:T(8,128)}, f32[9,32,32]{2,1,0:T(8,128)}, f32[1,32]{1,0:T(1,128)}) custom-call(bf16[32,128,128]{2,1,0:T(8,128)(2,1)} %get-tuple-element.13.pair, f32[10,8,128]{2,1,0:T(8,128)} %get-tuple-element.14.kres, f32[4,2,8,128]{3,2,1,0:T(8,128)} %get-tuple-element.15.rcres), custom_call_target="tpu_custom_call" | custom-call | tf_op jit(solution)/shard_map/finish_kernel/pallas_call | solution.py:523

commit v2 on v1

--- a/solution.py
+++ b/solution.py
@@ -43,9 +43,9 @@
     R, T, embed_scale, weight_scale,
     dilation, band, rows, cols, valid, kf, bias, cot,
     out, kres, rcres,
-    pack, blocks, cf, ct, edge_l, edge_r, from_r, from_l,
-    cw, nr, hlc, hlr, hact, hval,
-    act5, gz5, gzm, hid, der, vb, vb16, yz, yd, wz, wd, kacc, bacc, kg, row, col,
+    pack, blocks, cf, ct, edge_l, edge_r, from_r, from_l, top, bottom,
+    cw, rb, hlc, hlr, hpk, hval, um, ha, hg,
+    act5, gz5, gzm, hid, der, vb, vb16, yz, yd, wz, wd, kacc, csum, kg, row, col,
     kbuf, rbuf, abuf, bbuf, ksum, rcsum,
     ps, pr, hs, hr, ks, kr, rs, rr, as_, ar, bs, br, k2s, k2r, r2s, r2r,
 ):
@@ -118,8 +118,8 @@
         plan = (
             (left, edge_l, from_r.at[pl.ds(1, tiles)], 0, 0, -1),
             (right, edge_r, from_l.at[pl.ds(1, tiles)], 1, 0, 1),
-            (above, ct.at[pl.ds(m, m)], ct.at[pl.ds(n + m, m)], 2, -1, 0),
-            (below, ct.at[pl.ds(n, m)], ct.at[pl.ds(0, m)], 3, 1, 0),
+            (above, ct.at[pl.ds(m, m)], bottom, 2, -1, 0),
+            (below, ct.at[pl.ds(n, m)], top, 3, 1, 0),
             (below & left, edge_l.at[last], from_r.at[0], 4, 1, -1),
             (above & left, edge_l.at[0], from_r.at[tiles + 1], 5, -1, -1),
             (below & right, edge_r.at[last], from_l.at[0], 6, 1, 1),
@@ -135,6 +135,12 @@
         def _():
             c.start()
     halos(start)
+
+    for s in range(per):
+        p = lax.broadcasted_iota(jnp.int32, (2 * n, n), 0)
+        x = lax.broadcasted_iota(jnp.int32, (2 * n, n), 1)
+        pick = ((p == width * s + x) & (x < width)) | ((p == width * s + x + width) & (x >= n - width) & (p >= n))
+        um[:, s * n : (s + 1) * n] = jnp.where(pick, 1.0, 0.0).astype(bf)
 
     for a in range(3):
         zrow, drow = [None] * 5, [None] * 5
@@ -155,16 +161,14 @@
         x = blocks[q + t + k].astype(f32)
         cw[k, 0:ch] = x[0:ch]
         cw[k, ch : ch + RG] = x[v0 : v0 + RG]
-    for k in range(3):
-        x = blocks[q + k].astype(f32)
-        nr[k, 0:ch] = x[ch : 2 * ch]
-        nr[k, ch : ch + RG] = x[v0 : v0 + RG]
-
     hrows = ch + 16
     slots = tiles + 2
     lane_h = lax.broadcasted_iota(jnp.int32, (hrows, n), 1)
     cblk = [jnp.concatenate([blocks[q + t + k, 0:ch], blocks[q + t + k, v0 : v0 + 16]], axis=0) for k in range(4)]
     rblk = [jnp.concatenate([blocks[q + k, ch : 2 * ch], blocks[q + k, v0 : v0 + 16]], axis=0) for k in range(3)]
+
+    for k in range(3):
+        rb[k] = rblk[k]
 
     def window(blks, base):
         k, sh = base // n, base % n
@@ -193,99 +197,109 @@
             v = jnp.concatenate([v8] * (ch // RG), axis=0)
             h = (hrw[0:ch] + hcc[0:ch]) * v
             _, _, cdf = gelu_parts(h)
-            hact[side, g] = (h * cdf).astype(bf)
+            hpk[g * ch : (g + 1) * ch, side * n : (side + 1) * n] = (h * cdf).astype(bf)
             hval[side, g] = jnp.concatenate([v8, v8], axis=0).astype(bf)
 
     lane8 = lax.broadcasted_iota(jnp.int32, (RG, n), 1)
     lane40 = lax.broadcasted_iota(jnp.int32, (ch + RG, n), 1)
-
-    def shifts(dst, e, main, hright, hleft):
-        s = lax.rem(e + per - m, per)
-        a = pltpu.roll(hright, lax.rem(n - width * s, n), 1)
-        b = pltpu.roll(hleft, lax.rem(2 * n - width - width * s, n), 1)
-        hx = jnp.where(lane < n // 2, a, b)
-        dst[e, 2 * ch : 3 * ch] = main
-        for k in (1, 2):
-            sr = k * r
-            dst[e, (2 + k) * ch : (3 + k) * ch] = pltpu.roll(jnp.where(lane < sr, hx, main), n - sr, 1)
-            dst[e, (2 - k) * ch : (3 - k) * ch] = pltpu.roll(jnp.where(lane >= n - sr, hx, main), sr, 1)
-
-    def phase_a1(gi):
+    lane16 = lax.broadcasted_iota(jnp.int32, (16, n), 1)
+    sub16 = lax.broadcasted_iota(jnp.int32, (16, n), 0)
+
+    def unpack(dst):
+        for j in range(per // 2):
+            y = jnp.dot(hpk[...], um[:, 2 * j * n : 2 * (j + 1) * n], preferred_element_type=f32)
+            for g in range(slots):
+                for s in range(2):
+                    dst[g * per + 2 * j + s] = y[g * ch : (g + 1) * ch, s * n : (s + 1) * n].astype(bf)
+    unpack(ha)
+
+    def shifts(dst, halo, gi):
         for ii in range(RG):
             e = gi * RG + ii
-            at = e - m + n
+            hx, main = halo[e + per - m], dst[e, 2 * ch : 3 * ch]
+            for k in (1, 2):
+                sr = k * r
+                dst[e, (2 + k) * ch : (3 + k) * ch] = pltpu.roll(jnp.where(lane < sr, hx, main), n - sr, 1)
+                dst[e, (2 - k) * ch : (3 - k) * ch] = pltpu.roll(jnp.where(lane >= n - sr, hx, main), sr, 1)
+
+    ones = jnp.ones((n, n), bf)
+
+    def prep(gi):
+        picks, vrow, where_at = [], jnp.zeros((16, n), bf), []
+        for ii in range(RG):
+            at = gi * RG + ii - m + n
             k, sh = at // n, lax.rem(at, n)
-            c = pltpu.roll(jnp.where(lane40 >= sh, cw[k], cw[k + 1]), lax.rem(n - sh, n), 1)
-            rw = jnp.take_along_axis(nr[k], jnp.full((ch + RG, n), sh, jnp.int32), axis=1)
-            v8 = jnp.where(lane8 + d0 < w, c[ch:] * rw[ch:], 0.0)
+            where_at.append((k, sh))
+            x = rb[k]
+            picks.append(jnp.where(lane == sh, x[:ch], 0.0))
+            vrow = jnp.where((sub16 == ii) & (lane16 == sh), x[ch:], vrow)
+        rw = jnp.dot(jnp.concatenate(picks + [vrow], axis=0), ones, preferred_element_type=f32)
+        for ii in range(RG):
+            e = gi * RG + ii
+            k, sh = where_at[ii]
+            c = pltpu.roll(jnp.where(lane40 >= sh, cw[k], cw[k + 1]), (n - sh) & (n - 1), 1)
+            vr = rw[RG * ch + ii : RG * ch + ii + 1]
+            v8 = jnp.where(lane8 + d0 < w, c[ch:] * vr, 0.0)
             vb[e] = v8
-            vb16[e] = jnp.concatenate([v8, v8], axis=0).astype(bf)
-            v = jnp.concatenate([v8] * (ch // RG), axis=0)
-            h = (rw[:ch] + c[:ch]) * v
-            h2, tt, cdf = gelu_parts(h)
-            hid[e] = h
-            der[e] = (cdf + (0.5 * h) * (1.0 - tt * tt) * (S2PI + (3.0 * CUBIC * S2PI) * h2)) * v
-            slot = (e + per - m) // per
-            shifts(act5, e, (h * cdf).astype(bf), hact[0, slot], hact[1, slot])
-    loop(ext // RG, phase_a1)
-
-    def finish(ok, got, src, dst, c):
-        @pl.when(got)
-        def _():
-            c.wait_recv()
-
-        @pl.when(jnp.logical_not(got))
-        def _():
-            dst[...] = jnp.zeros(dst.shape, bf)
-    halos(finish)
-
-    def halo_gz(g):
-        for side, buf in ((0, from_r), (1, from_l)):
-            x = hval[side, g]
-            buf[g] = buf[g] * jnp.concatenate([x, x], axis=0)
-    loop(slots, halo_gz)
-    bacc[...] = jnp.zeros_like(bacc)
-    for e in range(2 * m):
-        gzm[e] = jnp.zeros((ch, n), bf)
-        gzm[n + 2 * m + e] = jnp.zeros((ch, n), bf)
-
-    def gz_row(e, inner):
-        x = vb16[e]
-        g = ct[e] * jnp.concatenate([x, x], axis=0)
-        slot = (e + per - m) // per
-        shifts(gz5, e, g, from_r[slot], from_l[slot])
-        if inner:
-            gzm[e + m] = g
-            return g.astype(f32)
-
-    def phase_a2(gi):
-        tot = bacc[...]
-        for ii in range(RG):
-            tot = tot + gz_row(m + gi * RG + ii, True)
-        bacc[...] = tot
-    loop(n // RG, phase_a2)
-
-    def outer_rows(s):
-        gz_row(s, False)
-        gz_row(n + m + s, False)
-    loop(m, outer_rows)
-
-    gr = divisor(ext, 34)
-    kacc[...] = jnp.zeros_like(kacc)
-
-    def phase_k(gi):
-        xs, gs, ys = [], [], []
-        for ii in range(gr):
-            e = gi * gr + ii
+            x = jnp.concatenate([v8, v8], axis=0).astype(bf)
+            vb16[e] = x
+            hid[e] = (rw[ii * ch : (ii + 1) * ch] + c[:ch]) * jnp.concatenate([v8] * (ch // RG), axis=0)
+            gzm[e + m] = ct[e] * jnp.concatenate([x, x], axis=0)
+
+    def gelus(gi):
+        for ii in range(RG):
+            e = gi * RG + ii
+            h = hid[e]
+            h2 = h * h
+            cdf = 0.5 + 0.5 * jnp.tanh(h * (S2PI + (S2PI * CUBIC) * h2))
+            act5[e, 2 * ch : 3 * ch] = (h * cdf).astype(bf)
+            x = h * (2.0 * S2PI + (6.0 * S2PI * CUBIC) * h2)
+            cv = cdf * jnp.concatenate([vb[e]] * (ch // RG), axis=0)
+            der[e] = cv + cv * ((1.0 - cdf) * x)
+
+    def kgrad(gi):
+        xs, gs = [], []
+        for ii in range(RG):
+            e = gi * RG + ii
             xs.append(act5[e])
-            ys.append(gz5[e])
             gs.append(jnp.concatenate([gzm[e + m - (a - 1) * r] for a in range(3)], axis=0))
         kacc[...] += lax.dot_general(jnp.concatenate(gs, axis=1), jnp.concatenate(xs, axis=1),
                                      (((1,), (1,)), ((), ())), preferred_element_type=f32)
-        y = jnp.dot(wd[...], jnp.concatenate(ys, axis=1), preferred_element_type=f32)
-        for ii in range(gr):
-            yd[gi * gr + ii] = y[:, ii * n : (ii + 1) * n]
-    loop(ext // gr, phase_k)
+
+    def pipeline(stages, counts, lags):
+        first_full = max(lags)
+        last_full = min(c + l for c, l in zip(counts, lags))
+        total = max(c + l for c, l in zip(counts, lags))
+
+        def at_step(j):
+            for f, c, l in zip(stages, counts, lags):
+                if 0 <= j - l < c:
+                    f(j - l)
+        for j in range(first_full):
+            at_step(j)
+
+        def body(j):
+            for f, l in zip(stages, lags):
+                f(j + first_full - l)
+        loop(last_full - first_full, body)
+        for j in range(last_full, total):
+            at_step(j)
+
+    ge, gm = ext // RG, n // RG
+    kacc[...] = jnp.zeros_like(kacc)
+    for e in range(m):
+        gzm[e] = jnp.zeros((ch, n), bf)
+        gzm[n + 3 * m + e] = jnp.zeros((ch, n), bf)
+    for e in range(m):
+        ct[e] = jnp.zeros((ch, n), bf)
+        ct[n + m + e] = jnp.zeros((ch, n), bf)
+    pipeline((kgrad, lambda g: shifts(act5, ha, g), gelus, prep), (ge,) * 4, (3, 2, 1, 0))
+
+    def bsums(gi, tot):
+        for ii in range(2 * RG):
+            tot = tot + gzm[2 * m + gi * 2 * RG + ii].astype(f32)
+        return tot
+    btot = lax.fori_loop(0, n // (2 * RG), bsums, jnp.zeros((ch, n), f32))
 
     for a in range(3):
         for b in range(3):
@@ -293,32 +307,80 @@
             x = kacc[a * ch : (a + 1) * ch, k * ch : (k + 1) * ch]
             kg[3 * a + b] = jnp.concatenate([x[z * RG : (z + 1) * RG] for z in range(ch // RG)], axis=1)
     diag = lax.broadcasted_iota(jnp.int32, (ch, n), 0) == lane
-    bt = jnp.sum(bacc[...], axis=1, keepdims=True)
+    bt = jnp.sum(btot, axis=1, keepdims=True)
     kg[9] = jnp.broadcast_to(jnp.sum(jnp.where(diag, bt, 0.0), axis=0, keepdims=True), (RG, n))
 
-    def phase_b(gi, carry):
-        lo, hi, rsum = carry
+    def k1(k):
+        return send(kg.at[k], kbuf.at[me], ks.at[k], kr.at[me], k // T, k % T)
+
+    def first_k(act):
+        for k in range(K):
+            @pl.when(me != k)
+            def _():
+                act(k1(k))
+    first_k(lambda c: c.start())
+
+    def finish(ok, got, src, dst, c):
+        @pl.when(got)
+        def _():
+            c.wait_recv()
+
+        @pl.when(jnp.logical_not(got))
+        def _():
+            dst[...] = jnp.zeros(dst.shape, bf)
+    halos(finish)
+
+    for g in range(slots):
+        for side, buf in ((0, from_r), (1, from_l)):
+            x = hval[side, g]
+            hpk[g * ch : (g + 1) * ch, side * n : (side + 1) * n] = buf[g] * jnp.concatenate([x, x], axis=0)
+    unpack(hg)
+    for e in range(m):
+        for buf, at in ((top, e), (bottom, n + m + e)):
+            x = vb16[at]
+            gz5[at, 2 * ch : 3 * ch] = buf[e] * jnp.concatenate([x, x], axis=0)
+
+    def gz_main(gi):
+        for ii in range(2 * RG):
+            e = m + gi * 2 * RG + ii
+            gz5[e, 2 * ch : 3 * ch] = gzm[e + m]
+    loop(n // (2 * RG), gz_main)
+
+    def conv_d(gi):
+        y = jnp.dot(wd[...], jnp.concatenate([gz5[gi * RG + ii] for ii in range(RG)], axis=1), preferred_element_type=f32)
+        for ii in range(RG):
+            yd[gi * RG + ii] = y[:, ii * n : (ii + 1) * n]
+
+    csum[...] = jnp.zeros_like(csum)
+
+    def backward(gi):
+        lo, hi = csum[0], csum[1]
         for ii in range(RG):
             i = gi * RG + ii
             da = yd[m + i + r, 0:ch] + yd[m + i, ch : 2 * ch] + yd[m + i - r, 2 * ch : 3 * ch]
             dx = gzm[i + 2 * m].astype(f32) + der[m + i] * da
+            der[m + i] = dx
             x = pltpu.roll(dx, i, 1)
             wrap = lane < i
             lo = lo + jnp.where(wrap, 0.0, x)
             hi = hi + jnp.where(wrap, x, 0.0)
-            rsum = jnp.where(lane == i, jnp.sum(dx, axis=1, keepdims=True), rsum)
-        return lo, hi, rsum
-    zf = jnp.zeros((ch, n), f32)
-    lo, hi, rsum = lax.fori_loop(0, n // RG, phase_b, (zf, zf, zf))
+        csum[0] = lo
+        csum[1] = hi
+    pipeline((backward, conv_d, lambda g: shifts(gz5, hg, g)), (gm, ge, ge), (3, 1, 0))
+    lo, hi = csum[0], csum[1]
+
+    def row_sums(gi, rsum):
+        for ii in range(2 * RG):
+            i = gi * 2 * RG + ii
+            rsum = jnp.where(lane == i, jnp.sum(der[m + i], axis=1, keepdims=True), rsum)
+        return rsum
+    rsum = lax.fori_loop(0, n // (2 * RG), row_sums, jnp.zeros((ch, n), f32))
     for z in range(Z):
         sl = slice(z * RG, (z + 1) * RG)
         row[z] = rsum[sl]
         col[0, z] = lo[sl]
         col[1, z] = hi[sl]
 
-    def k1(k):
-        return send(kg.at[k], kbuf.at[me], ks.at[k], kr.at[me], k // T, k % T)
-
     def r1(z):
         return send(row.at[z], rbuf.at[t], rs.at[z], rr.at[t], q, z)
 
@@ -329,10 +391,6 @@
         return send(col.at[1, z], bbuf.at[q], bs.at[z], br.at[q], q + t + 1, z)
 
     def first(act):
-        for k in range(K):
-            @pl.when(me != k)
-            def _():
-                act(k1(k))
         for z in range(Z):
             @pl.when(t != z)
             def _():
@@ -348,38 +406,13 @@
 
     first(lambda c: c.start())
 
-    def phase_z(gi):
-        x = jnp.concatenate([act5[gi * gr + ii] for ii in range(gr)], axis=1)
-        y = jnp.dot(wz[...], x, preferred_element_type=f32)
-        for ii in range(gr):
-            yz[gi * gr + ii] = y[:, ii * n : (ii + 1) * n]
-    loop(ext // gr, phase_z)
-    eye = lax.broadcasted_iota(jnp.int32, (ch, ch), 0) == lax.broadcasted_iota(jnp.int32, (ch, ch), 1)
-    bcol = jnp.sum(jnp.where(eye, bias[...], 0.0), axis=1, keepdims=True)
-    bias_all = jnp.broadcast_to(bcol, (ch, n))
-
-    def phase_o(gi):
-        for ii in range(RG):
-            i = gi * RG + ii
-            z = yz[m + i - r, 0:ch] + yz[m + i, ch : 2 * ch] + yz[m + i + r, 2 * ch : 3 * ch]
-            v = jnp.concatenate([vb[m + i]] * (ch // RG), axis=0)
-            cf[pl.ds(i, ch, stride=stride), :] = (hid[m + i] + z + bias_all) * v
-    loop(n // RG, phase_o)
-
-    def emit(c):
-        out[c] = cf[pl.ds(pl.multiple_of(c * stride, 8), n), :].astype(bf)
-    loop(ch, emit)
-
     def got(buf, sem):
         send(buf, buf, sem, sem, q, t).wait_recv()
 
     def k2(p):
         return send(ksum, kres.at[me], k2s.at[p], k2r.at[me], p // T, p % T)
 
-    def r2(p):
-        return send(rcsum, rcres.at[t], r2s.at[p], r2r.at[t], q, p)
-
-    def second(act):
+    def second_k(act):
         @pl.when(me < K)
         def _():
             def one(p):
@@ -388,6 +421,45 @@
                     act(k2(p))
             loop(N, one)
 
+    @pl.when(me < K)
+    def _():
+        ksum[...] = kg[me]
+
+        def take(p):
+            @pl.when(p != me)
+            def _():
+                got(kbuf.at[p], kr.at[p])
+                ksum[...] += kbuf[p]
+        loop(N, take)
+        ksum[...] = ksum[...] * weight_scale
+        kres[me] = ksum[...]
+    second_k(lambda c: c.start())
+
+    def conv_z(gi):
+        y = jnp.dot(wz[...], jnp.concatenate([act5[gi * RG + ii] for ii in range(RG)], axis=1), preferred_element_type=f32)
+        for ii in range(RG):
+            yz[gi * RG + ii] = y[:, ii * n : (ii + 1) * n]
+
+    eye = lax.broadcasted_iota(jnp.int32, (ch, ch), 0) == lax.broadcasted_iota(jnp.int32, (ch, ch), 1)
+    bcol = jnp.sum(jnp.where(eye, bias[...], 0.0), axis=1, keepdims=True)
+    bias_all = jnp.broadcast_to(bcol, (ch, n))
+
+    def phase_o(gi):
+        for ii in range(RG):
+            i = gi * RG + ii
+            z = yz[m + i - r, 0:ch] + yz[m + i, ch : 2 * ch] + yz[m + i + r, 2 * ch : 3 * ch]
+            v = jnp.concatenate([vb[m + i]] * (ch // RG), axis=0)
+            cf[pl.ds(i, ch, stride=stride), :] = (hid[m + i] + z + bias_all) * v
+    pipeline((phase_o, conv_z), (gm, ge), (2, 0))
+
+    def emit(c):
+        out[c] = cf[pl.ds(pl.multiple_of(c * stride, 8), n), :].astype(bf)
+    loop(ch, emit)
+
+    def r2(p):
+        return send(rcsum, rcres.at[t], r2s.at[p], r2r.at[t], q, p)
+
+    def second(act):
         @pl.when(t < Z)
         def _():
             def one(p):
@@ -396,19 +468,6 @@
                     act(r2(p))
             loop(T, one)
 
-    @pl.when(me < K)
-    def _():
-        ksum[...] = kg[me]
-
-        def take(p):
-            @pl.when(p != me)
-            def _():
-                got(kbuf.at[p], kr.at[p])
-                ksum[...] += kbuf[p]
-        loop(N, take)
-        ksum[...] = ksum[...] * weight_scale
-        kres[me] = ksum[...]
-
     @pl.when(t < Z)
     def _():
         rcsum[0] = row[t]
@@ -455,12 +514,15 @@
         def _():
             c.wait_send()
     halos(sent)
+    first_k(lambda c: c.wait_send())
     first(lambda c: c.wait_send())
+    second_k(lambda c: c.wait_send())
     second(lambda c: c.wait_send())
 
 
-def finish_kernel(pair, kres, rcres, out, row_out, col_out, kg_out, bg_out):
-    out[...] = pair[...]
+def finish_kernel(pair, kres, rcres, out, row_out, col_out, kg_out, bg_out, sem):
+    copy = pltpu.make_async_copy(pair, out, sem)
+    copy.start()
     ch = row_out.shape[0]
     for z in range(ch // RG):
         row_out[z * RG : (z + 1) * RG, :] = rcres[z, 0]
@@ -468,6 +530,7 @@
         for s in range(9):
             kg_out[s, z * RG : (z + 1) * RG, :] = kres[s, :, z * ch : (z + 1) * ch]
     bg_out[...] = kres[9, 0:1, 0:ch]
+    copy.wait()
 
 
 def local(emb_rows, emb_cols, kernel, bias, cotangent, valid, dilation, band):
@@ -494,23 +557,23 @@
     pair, kres, rcres = pl.pallas_call(
         functools.partial(fused_kernel, R, T, embed_scale, weight_scale),
         out_shape=(
-            jax.ShapeDtypeStruct((ch, n, n), bf),
-            jax.ShapeDtypeStruct((nk, RG, n), f32),
-            jax.ShapeDtypeStruct((Z, 2, RG, n), f32),
+            V((ch, n, n), bf),
+            V((nk, RG, n), f32),
+            V((Z, 2, RG, n), f32),
         ),
         in_specs=[smem, smem] + [vmem] * 6,
         out_specs=(vmem,) * 3,
         scratch_shapes=[
             V((2 * ch + 16, n), bf), V((R + T + 3, 2 * ch + 16, n), bf), V((ch * (n + 8), n), f32),
-            edges(ext), edges(tiles), edges(tiles), edges(slots), edges(slots),
-            V((4, ch + RG, n), f32), V((3, ch + RG, n), f32),
+            edges(ext), edges(tiles), edges(tiles), edges(slots), edges(slots), edges(m), edges(m),
+            V((4, ch + RG, n), f32), V((3, ch + 16, n), bf),
             V((slots * 2 * hrows, n), bf), V((slots * hrows, n), bf),
-            V((2, slots, ch, n), bf), V((2, slots, 16, n), bf),
+            V((slots * ch, 2 * n), bf), V((2, slots, 16, n), bf), V((2 * n, per * n), bf), edges(slots * per), edges(slots * per),
             V((ext, 5 * ch, n), bf), V((ext, 5 * ch, n), bf), V((ext + 2 * m, ch, n), bf),
             V((ext, ch, n), f32), V((ext, ch, n), f32), V((ext, RG, n), f32), V((ext, 16, n), bf),
             V((ext, 3 * ch, n), f32), V((ext, 3 * ch, n), f32),
             V((3 * ch, 5 * ch), bf), V((3 * ch, 5 * ch), bf), V((3 * ch, 5 * ch), f32),
-            V((ch, n), f32), tile(nk), tile(Z), tile(2, Z),
+            V((2, ch, n), f32), tile(nk), tile(Z), tile(2, Z),
             tile(R * T), tile(T), tile(R), tile(R), tile(), tile(2),
             dma((R,)), dma((R,)), dma((8,)), dma((8,)),
             dma((nk,)), dma((R * T,)), dma((Z,)), dma((T,)), dma((Z,)), dma((R,)), dma((Z,)), dma((R,)),
@@ -530,9 +593,10 @@
             jax.ShapeDtypeStruct((1, ch), f32),
         ),
         in_specs=[vmem] * 3,
-        out_specs=(vmem,) * 5,
+        out_specs=(pl.BlockSpec(memory_space=pl.ANY),) + (vmem,) * 4,
+        scratch_shapes=[pltpu.SemaphoreType.DMA],
         name="finish_kernel",
-    )(pair, kres, rcres)
+    )(*(pltpu.with_memory_space_constraint(x, V) for x in (pair, kres, rcres)))
     return out, row_grad, col_grad, kgt.reshape(3, 3, ch, ch), bgt.reshape(ch)
 
 

time: 46.6 us -> 34.6 us (0.74)
  Pallas kernels: 44.4 us -> 32.5 us
    pallas_call x1, Pallas kernels: 42.1 us -> 30.8 us  [local(): pl.pallas_call(functools.partial(fused_kernel, R, T, embed_scale, weight_...]
    pallas_call x1, Pallas kernels: 2.34 us -> 1.66 us  [local(): pl.pallas_call(finish_kernel, out_shape=(jax.ShapeDtypeStruct((ch, n, n),...]
where the time goes in v2:
time: 34.6 us; the launch traced here: 34.4 us
  Pallas kernels  32.5 us (94%)
  between operations  1.93 us (6%)
    pallas_call x1, Pallas kernels, local(): pl.pallas_call(functools.partial(fused_kernel, R, T, embed_scale, weight_...  30.8 us
    pallas_call x1, Pallas kernels, local(): pl.pallas_call(finish_kernel, out_shape=(jax.ShapeDtypeStruct((ch, n, n),...  1.66 us

profile of v2, /device:TPU:0, one launch (start us, length us, event | category | flops | bytes accessed | tf_op | source)
XLA Modules:
  0.0 34.4 jit_solution(3132723400913673662)
XLA Ops:
  1.9 30.8 %fused_kernel.1 = (bf16[32,128,128]{2,1,0:T(8,128)(2,1)S(1)}, f32[10,8,128]{2,1,0:T(8,128)S(1)}, f32[4,2,8,128]{3,2,1,0:T(8,128)S(1)}) custom-call(s32[1]{0:T(128)S(6)} %copy.13.dilation, s32[1]{0:T(128)S(6)} %copy.14.band, bf16[32,128]{1,0:T(8,128)(2,1)} %rows.1, bf16[32,128]{1,0:T(8,128)(2,1)} %cols.1, s32[1,128]{1,0:T(1,128)} %bitcast.6, ...), custom_call_target="tpu_custom_call" | custom-call | tf_op jit(solution)/shard_map/fused_kernel/pallas_call | solution.py:557
  32.7 1.7 %finish_kernel.1 = (bf16[32,128,128]{2,1,0:T(8,128)(2,1)}, f32[32,128]{1,0:T(8,128)}, f32[32,128]{1,0:T(8,128)}, f32[9,32,32]{2,1,0:T(8,128)}, f32[1,32]{1,0:T(1,128)}) custom-call(bf16[32,128,128]{2,1,0:T(8,128)(2,1)S(1)} %get-tuple-element.13.pair, f32[10,8,128]{2,1,0:T(8,128)S(1)} %get-tuple-element.14.kres, f32[4,2,8,128]{3,2,1,0:T(8,128)S(1)} %get-tuple-element.15.rcres), custom_call_target="tpu_custom_call" | custom-call | tf_op jit(solution)/shard_map/finish_kernel/pallas_call | solution.py:586

commit v3 on v2

--- a/solution.py
+++ b/solution.py
@@ -45,7 +45,7 @@
     out, kres, rcres,
     pack, blocks, cf, ct, edge_l, edge_r, from_r, from_l, top, bottom,
     cw, rb, hlc, hlr, hpk, hval, um, ha, hg,
-    act5, gz5, gzm, hid, der, vb, vb16, yz, yd, wz, wd, kacc, csum, kg, row, col,
+    act5, gz5, actm, hh, hid, der, vb, vb16, yz, yd, wz, wd, kacc, csum, kg, row, col,
     kbuf, rbuf, abuf, bbuf, ksum, rcsum,
     ps, pr, hs, hr, ks, kr, rs, rr, as_, ar, bs, br, k2s, k2r, r2s, r2r,
 ):
@@ -195,9 +195,7 @@
             da = d0 + kk + (-width if side else n)
             v8 = jnp.where((da >= 0) & (da < w), hcc[ch : ch + RG] * hrw[ch : ch + RG], 0.0)
             v = jnp.concatenate([v8] * (ch // RG), axis=0)
-            h = (hrw[0:ch] + hcc[0:ch]) * v
-            _, _, cdf = gelu_parts(h)
-            hpk[g * ch : (g + 1) * ch, side * n : (side + 1) * n] = (h * cdf).astype(bf)
+            hh[side, g] = (hrw[0:ch] + hcc[0:ch]) * v
             hval[side, g] = jnp.concatenate([v8, v8], axis=0).astype(bf)
 
     lane8 = lax.broadcasted_iota(jnp.int32, (RG, n), 1)
@@ -211,8 +209,6 @@
             for g in range(slots):
                 for s in range(2):
                     dst[g * per + 2 * j + s] = y[g * ch : (g + 1) * ch, s * n : (s + 1) * n].astype(bf)
-    unpack(ha)
-
     def shifts(dst, halo, gi):
         for ii in range(RG):
             e = gi * RG + ii
@@ -244,7 +240,7 @@
             x = jnp.concatenate([v8, v8], axis=0).astype(bf)
             vb16[e] = x
             hid[e] = (rw[ii * ch : (ii + 1) * ch] + c[:ch]) * jnp.concatenate([v8] * (ch // RG), axis=0)
-            gzm[e + m] = ct[e] * jnp.concatenate([x, x], axis=0)
+            gz5[e, 2 * ch : 3 * ch] = ct[e] * jnp.concatenate([x, x], axis=0)
 
     def gelus(gi):
         for ii in range(RG):
@@ -252,7 +248,9 @@
             h = hid[e]
             h2 = h * h
             cdf = 0.5 + 0.5 * jnp.tanh(h * (S2PI + (S2PI * CUBIC) * h2))
-            act5[e, 2 * ch : 3 * ch] = (h * cdf).astype(bf)
+            act = (h * cdf).astype(bf)
+            act5[e, 2 * ch : 3 * ch] = act
+            actm[e + m] = act
             x = h * (2.0 * S2PI + (6.0 * S2PI * CUBIC) * h2)
             cv = cdf * jnp.concatenate([vb[e]] * (ch // RG), axis=0)
             der[e] = cv + cv * ((1.0 - cdf) * x)
@@ -261,8 +259,8 @@
         xs, gs = [], []
         for ii in range(RG):
             e = gi * RG + ii
-            xs.append(act5[e])
-            gs.append(jnp.concatenate([gzm[e + m - (a - 1) * r] for a in range(3)], axis=0))
+            gs.append(gz5[e])
+            xs.append(jnp.concatenate([actm[e + m + (a - 1) * r] for a in range(3)], axis=0))
         kacc[...] += lax.dot_general(jnp.concatenate(gs, axis=1), jnp.concatenate(xs, axis=1),
                                      (((1,), (1,)), ((), ())), preferred_element_type=f32)
 
@@ -288,37 +286,18 @@
     ge, gm = ext // RG, n // RG
     kacc[...] = jnp.zeros_like(kacc)
     for e in range(m):
-        gzm[e] = jnp.zeros((ch, n), bf)
-        gzm[n + 3 * m + e] = jnp.zeros((ch, n), bf)
-    for e in range(m):
         ct[e] = jnp.zeros((ch, n), bf)
         ct[n + m + e] = jnp.zeros((ch, n), bf)
-    pipeline((kgrad, lambda g: shifts(act5, ha, g), gelus, prep), (ge,) * 4, (3, 2, 1, 0))
+    pipeline((gelus, prep), (ge,) * 2, (1, 0))
+    for e in range(2 * m):
+        actm[e] = jnp.zeros((ch, n), bf)
+        actm[n + 2 * m + e] = jnp.zeros((ch, n), bf)
 
     def bsums(gi, tot):
         for ii in range(2 * RG):
-            tot = tot + gzm[2 * m + gi * 2 * RG + ii].astype(f32)
+            tot = tot + gz5[m + gi * 2 * RG + ii, 2 * ch : 3 * ch].astype(f32)
         return tot
     btot = lax.fori_loop(0, n // (2 * RG), bsums, jnp.zeros((ch, n), f32))
-
-    for a in range(3):
-        for b in range(3):
-            k = b - a + 2
-            x = kacc[a * ch : (a + 1) * ch, k * ch : (k + 1) * ch]
-            kg[3 * a + b] = jnp.concatenate([x[z * RG : (z + 1) * RG] for z in range(ch // RG)], axis=1)
-    diag = lax.broadcasted_iota(jnp.int32, (ch, n), 0) == lane
-    bt = jnp.sum(btot, axis=1, keepdims=True)
-    kg[9] = jnp.broadcast_to(jnp.sum(jnp.where(diag, bt, 0.0), axis=0, keepdims=True), (RG, n))
-
-    def k1(k):
-        return send(kg.at[k], kbuf.at[me], ks.at[k], kr.at[me], k // T, k % T)
-
-    def first_k(act):
-        for k in range(K):
-            @pl.when(me != k)
-            def _():
-                act(k1(k))
-    first_k(lambda c: c.start())
 
     def finish(ok, got, src, dst, c):
         @pl.when(got)
@@ -340,12 +319,6 @@
             x = vb16[at]
             gz5[at, 2 * ch : 3 * ch] = buf[e] * jnp.concatenate([x, x], axis=0)
 
-    def gz_main(gi):
-        for ii in range(2 * RG):
-            e = m + gi * 2 * RG + ii
-            gz5[e, 2 * ch : 3 * ch] = gzm[e + m]
-    loop(n // (2 * RG), gz_main)
-
     def conv_d(gi):
         y = jnp.dot(wd[...], jnp.concatenate([gz5[gi * RG + ii] for ii in range(RG)], axis=1), preferred_element_type=f32)
         for ii in range(RG):
@@ -358,7 +331,7 @@
         for ii in range(RG):
             i = gi * RG + ii
             da = yd[m + i + r, 0:ch] + yd[m + i, ch : 2 * ch] + yd[m + i - r, 2 * ch : 3 * ch]
-            dx = gzm[i + 2 * m].astype(f32) + der[m + i] * da
+            dx = gz5[m + i, 2 * ch : 3 * ch].astype(f32) + der[m + i] * da
             der[m + i] = dx
             x = pltpu.roll(dx, i, 1)
             wrap = lane < i
@@ -366,7 +339,26 @@
             hi = hi + jnp.where(wrap, x, 0.0)
         csum[0] = lo
         csum[1] = hi
-    pipeline((backward, conv_d, lambda g: shifts(gz5, hg, g)), (gm, ge, ge), (3, 1, 0))
+    pipeline((backward, kgrad, conv_d, lambda g: shifts(gz5, hg, g)), (gm, ge, ge, ge), (3, 1, 1, 0))
+    for a in range(3):
+        for b in range(3):
+            k = a - b + 2
+            x = kacc[k * ch : (k + 1) * ch, a * ch : (a + 1) * ch]
+            kg[3 * a + b] = jnp.concatenate([x[z * RG : (z + 1) * RG] for z in range(ch // RG)], axis=1)
+    diag = lax.broadcasted_iota(jnp.int32, (ch, n), 0) == lane
+    bt = jnp.sum(btot, axis=1, keepdims=True)
+    kg[9] = jnp.broadcast_to(jnp.sum(jnp.where(diag, bt, 0.0), axis=0, keepdims=True), (RG, n))
+
+    def k1(k):
+        return send(kg.at[k], kbuf.at[me], ks.at[k], kr.at[me], k // T, k % T)
+
+    def first_k(act):
+        for k in range(K):
+            @pl.when(me != k)
+            def _():
+                act(k1(k))
+    first_k(lambda c: c.start())
+
     lo, hi = csum[0], csum[1]
 
     def row_sums(gi, rsum):
@@ -381,22 +373,25 @@
         col[0, z] = lo[sl]
         col[1, z] = hi[sl]
 
+    def root(z):
+        return (T - 2) // 2 + z % 2 if T > 1 else 0
+
     def r1(z):
-        return send(row.at[z], rbuf.at[t], rs.at[z], rr.at[t], q, z)
+        return send(row.at[z], rbuf.at[z, t], rs.at[z], rr.at[z, t], q, root(z))
 
     def a1(z):
-        return send(col.at[0, z], abuf.at[q], as_.at[z], ar.at[q], q + t, z)
+        return send(col.at[0, z], abuf.at[z, q], as_.at[z], ar.at[z, q], q + t, root(z))
 
     def b1(z):
-        return send(col.at[1, z], bbuf.at[q], bs.at[z], br.at[q], q + t + 1, z)
+        return send(col.at[1, z], bbuf.at[z, q], bs.at[z], br.at[z, q], q + t + 1, root(z))
 
     def first(act):
         for z in range(Z):
-            @pl.when(t != z)
+            @pl.when(t != root(z))
             def _():
                 act(r1(z))
 
-            @pl.when((q + t < R) & ((t != 0) | (z != 0)))
+            @pl.when((q + t < R) & ((t != 0) | (root(z) != 0)))
             def _():
                 act(a1(z))
 
@@ -405,6 +400,21 @@
                 act(b1(z))
 
     first(lambda c: c.start())
+
+    for g in range(slots):
+        for side in range(2):
+            h = hh[side, g]
+            _, _, cdf = gelu_parts(h)
+            hpk[g * ch : (g + 1) * ch, side * n : (side + 1) * n] = (h * cdf).astype(bf)
+    unpack(ha)
+    loop(ge, lambda g: shifts(act5, ha, g))
+
+    gr = divisor(ext, 34)
+
+    def conv_z(gi):
+        y = jnp.dot(wz[...], jnp.concatenate([act5[gi * gr + ii] for ii in range(gr)], axis=1), preferred_element_type=f32)
+        for ii in range(gr):
+            yz[gi * gr + ii] = y[:, ii * n : (ii + 1) * n]
 
     def got(buf, sem):
         send(buf, buf, sem, sem, q, t).wait_recv()
@@ -420,6 +430,51 @@
                 def _():
                     act(k2(p))
             loop(N, one)
+
+    def r2(z, p):
+        return send(rcsum.at[z], rcres.at[z], r2s.at[z, p], r2r.at[z], q, p)
+
+    def second(act):
+        for z in range(Z):
+            @pl.when(t == root(z))
+            def _():
+                def one(p):
+                    @pl.when(p != t)
+                    def _():
+                        act(r2(z, p))
+                loop(T, one)
+
+    for z in range(Z):
+        @pl.when(t == root(z))
+        def _():
+            rcsum[z, 0] = row[z]
+            rcsum[z, 1] = jnp.zeros((RG, n), f32)
+
+            def take(p):
+                @pl.when(p != t)
+                def _():
+                    got(rbuf.at[z, p], rr.at[z, p])
+                    rcsum[z, 0] += rbuf[z, p]
+            loop(T, take)
+
+            @pl.when(t == 0)
+            def _():
+                rcsum[z, 1] = col[0, z]
+
+            def take_col(p):
+                @pl.when((p <= q) & (q - p < T) & ((p != q) | (t != 0)))
+                def _():
+                    got(abuf.at[z, p], ar.at[z, p])
+                    rcsum[z, 1] += abuf[z, p]
+
+                @pl.when((p <= q - 1) & (q - 1 - p < T))
+                def _():
+                    got(bbuf.at[z, p], br.at[z, p])
+                    rcsum[z, 1] += bbuf[z, p]
+            loop(R, take_col)
+            rcsum[z] = rcsum[z] * embed_scale
+            rcres[z] = rcsum[z]
+    second(lambda c: c.start())
 
     @pl.when(me < K)
     def _():
@@ -434,11 +489,7 @@
         ksum[...] = ksum[...] * weight_scale
         kres[me] = ksum[...]
     second_k(lambda c: c.start())
-
-    def conv_z(gi):
-        y = jnp.dot(wz[...], jnp.concatenate([act5[gi * RG + ii] for ii in range(RG)], axis=1), preferred_element_type=f32)
-        for ii in range(RG):
-            yz[gi * RG + ii] = y[:, ii * n : (ii + 1) * n]
+    loop(ext // gr, conv_z)
 
     eye = lax.broadcasted_iota(jnp.int32, (ch, ch), 0) == lax.broadcasted_iota(jnp.int32, (ch, ch), 1)
     bcol = jnp.sum(jnp.where(eye, bias[...], 0.0), axis=1, keepdims=True)
@@ -450,61 +501,18 @@
             z = yz[m + i - r, 0:ch] + yz[m + i, ch : 2 * ch] + yz[m + i + r, 2 * ch : 3 * ch]
             v = jnp.concatenate([vb[m + i]] * (ch // RG), axis=0)
             cf[pl.ds(i, ch, stride=stride), :] = (hid[m + i] + z + bias_all) * v
-    pipeline((phase_o, conv_z), (gm, ge), (2, 0))
+    loop(gm, phase_o)
 
     def emit(c):
         out[c] = cf[pl.ds(pl.multiple_of(c * stride, 8), n), :].astype(bf)
     loop(ch, emit)
 
-    def r2(p):
-        return send(rcsum, rcres.at[t], r2s.at[p], r2r.at[t], q, p)
-
-    def second(act):
-        @pl.when(t < Z)
-        def _():
-            def one(p):
-                @pl.when(p != t)
-                def _():
-                    act(r2(p))
-            loop(T, one)
-
-    @pl.when(t < Z)
-    def _():
-        rcsum[0] = row[t]
-        rcsum[1] = jnp.zeros_like(rcsum[1])
-
-        def take(p):
-            @pl.when(p != t)
-            def _():
-                got(rbuf.at[p], rr.at[p])
-                rcsum[0] += rbuf[p]
-        loop(T, take)
-
-        @pl.when(t == 0)
-        def _():
-            rcsum[1] = col[0, 0]
-
-        def take_col(p):
-            @pl.when((p <= q) & (q - p < T) & ((p != q) | (t != 0)))
-            def _():
-                got(abuf.at[p], ar.at[p])
-                rcsum[1] += abuf[p]
-
-            @pl.when((p <= q - 1) & (q - 1 - p < T))
-            def _():
-                got(bbuf.at[p], br.at[p])
-                rcsum[1] += bbuf[p]
-        loop(R, take_col)
-        rcsum[...] = rcsum[...] * embed_scale
-        rcres[t] = rcsum[...]
-
-    second(lambda c: c.start())
     for k in range(K):
         @pl.when(me != k)
         def _():
             got(kres.at[k], k2r.at[k])
     for z in range(Z):
-        @pl.when(t != z)
+        @pl.when(t != root(z))
         def _():
             got(rcres.at[z], r2r.at[z])
     peers(lambda p: p1(p).wait_send())
@@ -520,9 +528,8 @@
     second(lambda c: c.wait_send())
 
 
-def finish_kernel(pair, kres, rcres, out, row_out, col_out, kg_out, bg_out, sem):
-    copy = pltpu.make_async_copy(pair, out, sem)
-    copy.start()
+def finish_kernel(pair, kres, rcres, out, row_out, col_out, kg_out, bg_out):
+    out[...] = pair[...]
     ch = row_out.shape[0]
     for z in range(ch // RG):
         row_out[z * RG : (z + 1) * RG, :] = rcres[z, 0]
@@ -530,7 +537,6 @@
         for s in range(9):
             kg_out[s, z * RG : (z + 1) * RG, :] = kres[s, :, z * ch : (z + 1) * ch]
     bg_out[...] = kres[9, 0:1, 0:ch]
-    copy.wait()
 
 
 def local(emb_rows, emb_cols, kernel, bias, cotangent, valid, dilation, band):
@@ -569,15 +575,15 @@
             V((4, ch + RG, n), f32), V((3, ch + 16, n), bf),
             V((slots * 2 * hrows, n), bf), V((slots * hrows, n), bf),
             V((slots * ch, 2 * n), bf), V((2, slots, 16, n), bf), V((2 * n, per * n), bf), edges(slots * per), edges(slots * per),
-            V((ext, 5 * ch, n), bf), V((ext, 5 * ch, n), bf), V((ext + 2 * m, ch, n), bf),
+            V((ext, 5 * ch, n), bf), V((ext, 5 * ch, n), bf), V((ext + 2 * m, ch, n), bf), V((2, slots, ch, n), f32),
             V((ext, ch, n), f32), V((ext, ch, n), f32), V((ext, RG, n), f32), V((ext, 16, n), bf),
             V((ext, 3 * ch, n), f32), V((ext, 3 * ch, n), f32),
-            V((3 * ch, 5 * ch), bf), V((3 * ch, 5 * ch), bf), V((3 * ch, 5 * ch), f32),
+            V((3 * ch, 5 * ch), bf), V((3 * ch, 5 * ch), bf), V((5 * ch, 3 * ch), f32),
             V((2, ch, n), f32), tile(nk), tile(Z), tile(2, Z),
-            tile(R * T), tile(T), tile(R), tile(R), tile(), tile(2),
+            tile(R * T), tile(Z, T), tile(Z, R), tile(Z, R), tile(), tile(Z, 2),
             dma((R,)), dma((R,)), dma((8,)), dma((8,)),
-            dma((nk,)), dma((R * T,)), dma((Z,)), dma((T,)), dma((Z,)), dma((R,)), dma((Z,)), dma((R,)),
-            dma((R * T,)), dma((nk,)), dma((T,)), dma((Z,)),
+            dma((nk,)), dma((R * T,)), dma((Z,)), dma((Z, T)), dma((Z,)), dma((Z, R)), dma((Z,)), dma((Z, R)),
+            dma((R * T,)), dma((nk,)), dma((Z, T)), dma((Z,)),
         ],
         compiler_params=pltpu.CompilerParams(collective_id=0, has_side_effects=True, vmem_limit_bytes=56 * 2**20),
         name="fused_kernel",
@@ -593,8 +599,7 @@
             jax.ShapeDtypeStruct((1, ch), f32),
         ),
         in_specs=[vmem] * 3,
-        out_specs=(pl.BlockSpec(memory_space=pl.ANY),) + (vmem,) * 4,
-        scratch_shapes=[pltpu.SemaphoreType.DMA],
+        out_specs=(vmem,) * 5,
         name="finish_kernel",
     )(*(pltpu.with_memory_space_constraint(x, V) for x in (pair, kres, rcres)))
     return out, row_grad, col_grad, kgt.reshape(3, 3, ch, ch), bgt.reshape(ch)

time: 34.6 us -> 34 us (0.983)
  Pallas kernels: 32.5 us -> 31.8 us
    pallas_call x1, Pallas kernels: 1.66 us -> 1.09 us  [local(): pl.pallas_call(finish_kernel, out_shape=(jax.ShapeDtypeStruct((ch, n, n),...]
where the time goes in v3:
time: 34 us; the launch traced here: 33.8 us
  Pallas kernels  31.8 us (94%)
  between operations  1.93 us (6%)
    pallas_call x1, Pallas kernels, local(): pl.pallas_call(functools.partial(fused_kernel, R, T, embed_scale, weight_...  30.7 us
    pallas_call x1, Pallas kernels, local(): pl.pallas_call(finish_kernel, out_shape=(jax.ShapeDtypeStruct((ch, n, n),...  1.09 us

profile of v3, /device:TPU:0, one launch (start us, length us, event | category | flops | bytes accessed | tf_op | source)
XLA Modules:
  0.0 33.8 jit_solution(6181965618209937417)
XLA Ops:
  1.9 30.7 %fused_kernel.1 = (bf16[32,128,128]{2,1,0:T(8,128)(2,1)S(1)}, f32[10,8,128]{2,1,0:T(8,128)S(1)}, f32[4,2,8,128]{3,2,1,0:T(8,128)S(1)}) custom-call(s32[1]{0:T(128)S(6)} %copy.13.dilation, s32[1]{0:T(128)S(6)} %copy.14.band, bf16[32,128]{1,0:T(8,128)(2,1)} %rows.1, bf16[32,128]{1,0:T(8,128)(2,1)} %cols.1, s32[1,128]{1,0:T(1,128)} %bitcast.6, ...), custom_call_target="tpu_custom_call" | custom-call | tf_op jit(solution)/shard_map/fused_kernel/pallas_call | solution.py:563
  32.7 1.1 %finish_kernel.1 = (bf16[32,128,128]{2,1,0:T(8,128)(2,1)}, f32[32,128]{1,0:T(8,128)}, f32[32,128]{1,0:T(8,128)}, f32[9,32,32]{2,1,0:T(8,128)}, f32[1,32]{1,0:T(1,128)}) custom-call(bf16[32,128,128]{2,1,0:T(8,128)(2,1)S(1)} %get-tuple-element.13.pair, f32[10,8,128]{2,1,0:T(8,128)S(1)} %get-tuple-element.14.kres, f32[4,2,8,128]{3,2,1,0:T(8,128)S(1)} %get-tuple-element.15.rcres), custom_call_target="tpu_custom_call" | custom-call | tf_op jit(solution)/shard_map/finish_kernel/pallas_call | solution.py:592

commit v4 on v3

--- a/solution.py
+++ b/solution.py
@@ -41,13 +41,13 @@
 
 def fused_kernel(
     R, T, embed_scale, weight_scale,
-    dilation, band, rows, cols, valid, kf, bias, cot,
+    dilation, band, rows, cols, valid, kf, bias, cot_hbm,
     out, kres, rcres,
     pack, blocks, cf, ct, edge_l, edge_r, from_r, from_l, top, bottom,
     cw, rb, hlc, hlr, hpk, hval, um, ha, hg,
     act5, gz5, actm, hh, hid, der, vb, vb16, yz, yd, wz, wd, kacc, csum, kg, row, col,
     kbuf, rbuf, abuf, bbuf, ksum, rcsum,
-    ps, pr, hs, hr, ks, kr, rs, rr, as_, ar, bs, br, k2s, k2r, r2s, r2r,
+    cot, cs, ps, pr, hs, hr, ks, kr, rs, rr, as_, ar, bs, br, k2s, k2r, r2s, r2r,
 ):
     ch, n = rows.shape
     m = MAXDIL
@@ -62,6 +62,8 @@
     me = q * T + t
     r, w = dilation[0], band[0]
     mesh_id = pl.DeviceIdType.MESH
+    load = pltpu.make_async_copy(cot_hbm, cot, cs)
+    load.start()
     barrier = pltpu.get_barrier_semaphore()
     left, right, above, below = t > 0, t < T - 1, q > 0, q < R - 1
 
@@ -96,6 +98,7 @@
 
     def spread(c):
         cf[pl.ds(pl.multiple_of(c * stride, 8), n), :] = cot[c].astype(f32)
+    load.wait()
     loop(ch, spread)
 
     def pack_edges(g):
@@ -567,7 +570,7 @@
             V((nk, RG, n), f32),
             V((Z, 2, RG, n), f32),
         ),
-        in_specs=[smem, smem] + [vmem] * 6,
+        in_specs=[smem, smem] + [vmem] * 5 + [pl.BlockSpec(memory_space=pl.ANY)],
         out_specs=(vmem,) * 3,
         scratch_shapes=[
             V((2 * ch + 16, n), bf), V((R + T + 3, 2 * ch + 16, n), bf), V((ch * (n + 8), n), f32),
@@ -581,7 +584,7 @@
             V((3 * ch, 5 * ch), bf), V((3 * ch, 5 * ch), bf), V((5 * ch, 3 * ch), f32),
             V((2, ch, n), f32), tile(nk), tile(Z), tile(2, Z),
             tile(R * T), tile(Z, T), tile(Z, R), tile(Z, R), tile(), tile(Z, 2),
-            dma((R,)), dma((R,)), dma((8,)), dma((8,)),
+            V((ch, n, n), bf), dma, dma((R,)), dma((R,)), dma((8,)), dma((8,)),
             dma((nk,)), dma((R * T,)), dma((Z,)), dma((Z, T)), dma((Z,)), dma((Z, R)), dma((Z,)), dma((Z, R)),
             dma((R * T,)), dma((nk,)), dma((Z, T)), dma((Z,)),
         ],

time: 34 us -> 33.5 us (0.985)
  Pallas kernels: 31.8 us -> 31.4 us
    pallas_call x1, Pallas kernels: 30.7 us -> 30.3 us  [local(): pl.pallas_call(functools.partial(fused_kernel, R, T, embed_scale, weight_...]
where the time goes in v4:
time: 33.5 us; the launch traced here: 33.3 us
  Pallas kernels  31.4 us (94%)
  between operations  1.93 us (6%)
    pallas_call x1, Pallas kernels, local(): pl.pallas_call(functools.partial(fused_kernel, R, T, embed_scale, weight_...  30.3 us
    pallas_call x1, Pallas kernels, local(): pl.pallas_call(finish_kernel, out_shape=(jax.ShapeDtypeStruct((ch, n, n),...  1.09 us

profile of v4, /device:TPU:0, one launch (start us, length us, event | category | flops | bytes accessed | tf_op | source)
XLA Modules:
  0.0 33.3 jit_solution(17584615200395577627)
XLA Ops:
  1.9 30.3 %fused_kernel.1 = (bf16[32,128,128]{2,1,0:T(8,128)(2,1)S(1)}, f32[10,8,128]{2,1,0:T(8,128)S(1)}, f32[4,2,8,128]{3,2,1,0:T(8,128)S(1)}) custom-call(s32[1]{0:T(128)S(6)} %copy.13.dilation, s32[1]{0:T(128)S(6)} %copy.14.band, bf16[32,128]{1,0:T(8,128)(2,1)} %rows.1, bf16[32,128]{1,0:T(8,128)(2,1)} %cols.1, s32[1,128]{1,0:T(1,128)} %bitcast.6, ...), custom_call_target="tpu_custom_call" | custom-call | tf_op jit(solution)/shard_map/fused_kernel/pallas_call | solution.py:566
  32.2 1.1 %finish_kernel.1 = (bf16[32,128,128]{2,1,0:T(8,128)(2,1)}, f32[32,128]{1,0:T(8,128)}, f32[32,128]{1,0:T(8,128)}, f32[9,32,32]{2,1,0:T(8,128)}, f32[1,32]{1,0:T(1,128)}) custom-call(bf16[32,128,128]{2,1,0:T(8,128)(2,1)S(1)} %get-tuple-element.13.pair, f32[10,8,128]{2,1,0:T(8,128)S(1)} %get-tuple-element.14.kres, f32[4,2,8,128]{3,2,1,0:T(8,128)S(1)} %get-tuple-element.15.rcres), custom_call_target="tpu_custom_call" | custom-call | tf_op jit(solution)/shard_map/finish_kernel/pallas_call | solution.py:595
